TPU v7x, 32 devices: a whole 2x2x4 slice. The times are simulated.
32 devices in a mesh: gx: 16 (over z, y, x), gy: 2 (over core).
Axes of the slice: x: 2, y: 2, z: 4, core: 2. Of those that a mesh axis runs over, the one named last changes fastest.
Arguments:
- sources: bfloat16 [2048, 8, 128], P(('gx', 'gy')), may hold values from -6 to 6
- owners: int32 [2048, 1], P(('gx', 'gy')), may hold values from 0 to 15; in each aligned block of 64 rows (0 to 63, 64 to 127, ...) at most 8 rows name the same one
- strip_rows: int32 [2048], P(('gx', 'gy')), may hold values from 0 to 255
- panel_counts: int32 [2048], P(('gx', 'gy')), may hold values from 1 to 128
- arrival_bins: int32 [4096, 4, 128], P('gx'), may hold values from 0 to 254
- arrival_fracs: float32 [4096, 4, 128], P('gx'), may hold values from 0 to 1
- gain_table: bfloat16 [4096, 8, 4, 1024], P('gx'), may hold values from -0.125 to 0.125
Outputs:
- signals: float32 [1024, 4, 256], P(('gx', 'gy'))
Inputs may be any that keep to these rules, and one draw needn't show every extreme that they name: `owners`: among the rows of one device, at most 8 strips name one patch, a bound that some block reaches.
All inputs are finite; a program needn't handle non-finite values.
Results may differ from a plain program's by a relative error of at most 0.0044.
Values may be sent and summed in bfloat16 or wider, within the bound.
A program may use at most 768 MiB of HBM per device.

v0:
```python
import functools

import jax
import jax.numpy as jnp
from jax import lax
from jax.experimental import pallas as pl
from jax.experimental.pallas import tpu as pltpu
from jax.sharding import PartitionSpec as P

NBIN = 256


def bin_kernel(block_ref, src_ref, bins_ref, fracs_ref, out_ref):
    block = block_ref[0]
    pairs = src_ref.shape[0] // 16
    panels = src_ref.shape[1]
    low = lax.broadcasted_iota(jnp.int32, (16, panels), 0) < 8
    spots = lax.broadcasted_iota(jnp.int32, (NBIN, panels), 0).astype(jnp.float32).astype(jnp.bfloat16)

    def weights_of(row):
        bins = bins_ref[row, pl.ds(block, 1), :].astype(jnp.float32)
        fracs = fracs_ref[row, pl.ds(block, 1), :]

        def spread(v):
            return jnp.broadcast_to(v, (NBIN, panels)).astype(jnp.bfloat16)

        first, second = spread(bins), spread(bins + 1.0)
        return jnp.where(
            spots == first,
            spread(1.0 - fracs),
            jnp.where(spots == second, spread(fracs), jnp.zeros((), jnp.bfloat16)),
        )

    def step(i, carry):
        both = src_ref[pl.ds(pl.multiple_of(i * 16, 16), 16), :].astype(jnp.float32)
        top = jnp.where(low, both, 0.0).astype(jnp.bfloat16)
        bottom = jnp.where(low, 0.0, both).astype(jnp.bfloat16)
        lhs = jnp.concatenate([top, bottom], axis=1)
        weights = jnp.concatenate([weights_of(2 * i), weights_of(2 * i + 1)], axis=1)
        got = lax.dot_general(
            lhs, weights, (((1,), (1,)), ((), ())), preferred_element_type=jnp.float32
        )
        out_ref[pl.ds(pl.multiple_of(i * 16, 16), 16), :] = got.astype(jnp.bfloat16)
        return carry

    lax.fori_loop(0, pairs, step, 0, unroll=4)


def bin_rows(block, src, bins, fracs):
    rows = src.shape[0]
    return pl.pallas_call(
        bin_kernel,
        out_shape=jax.ShapeDtypeStruct((rows, NBIN), jnp.bfloat16),
        in_specs=[
            pl.BlockSpec(memory_space=pltpu.SMEM),
            pl.BlockSpec(memory_space=pltpu.VMEM),
            pl.BlockSpec(memory_space=pltpu.VMEM),
            pl.BlockSpec(memory_space=pltpu.VMEM),
        ],
        out_specs=pl.BlockSpec(memory_space=pltpu.VMEM),
        name="bin_rows",
        cost_estimate=pl.CostEstimate(flops=rows * 2 * 256 * 256, bytes_accessed=rows * 1000, transcendentals=0),
    )(block, src, bins, fracs)


def on_device(sources, owners, strip_rows, panel_counts, arrival_bins, arrival_fracs, gain_table):
    strip_count, terms, panels = sources.shape
    shards = lax.axis_size("gx")
    columns = lax.axis_size("gy")
    capacity = 2 * strip_count // shards
    blocks = arrival_bins.shape[1]
    observers = gain_table.shape[3]
    rows_here = arrival_bins.shape[0]
    live_mask = (jnp.arange(panels, dtype=jnp.int32)[None, :] < panel_counts[:, None]).astype(
        jnp.bfloat16
    )
    masked = (sources * live_mask[:, None, :]).reshape(strip_count, terms * panels)
    lane = jnp.arange(128, dtype=jnp.int32)[None, :]
    coded = jnp.where(
        lane == 0,
        (strip_rows // 128)[:, None],
        jnp.where(lane == 1, (strip_rows % 128)[:, None], jnp.where(lane == 2, 1, 0)),
    ).astype(jnp.bfloat16)
    payload = jnp.concatenate([masked, coded], axis=1)
    targets = owners[:, 0]
    earlier = (
        jnp.arange(strip_count, dtype=jnp.int32)[None, :]
        < jnp.arange(strip_count, dtype=jnp.int32)[:, None]
    )
    order_in = jnp.sum(
        jnp.where(earlier & (targets[None, :] == targets[:, None]), 1, 0).astype(jnp.int32), axis=1
    )
    slot_of = targets * capacity + order_in
    placing = jnp.arange(shards * capacity, dtype=jnp.int32)[:, None] == slot_of[None, :]
    send = jnp.dot(
        placing.astype(jnp.bfloat16), payload, preferred_element_type=jnp.float32
    ).astype(jnp.bfloat16)
    got = lax.all_to_all(send, "gx", split_axis=0, concat_axis=0, tiled=True)
    got = lax.all_gather(got, "gy", axis=0, tiled=True)
    codes = got[:, terms * panels :].astype(jnp.int32)
    got_rows = jnp.where(codes[:, 2] > 0, codes[:, 0] * 128 + codes[:, 1], -1)
    row_hot = (jnp.arange(rows_here, dtype=jnp.int32)[:, None] == got_rows[None, :]).astype(
        jnp.bfloat16
    )
    row_sources = jnp.dot(
        row_hot, got[:, : terms * panels], preferred_element_type=jnp.float32
    ).astype(jnp.bfloat16)
    src = row_sources.reshape(rows_here * terms, panels)
    per = blocks // columns
    first = lax.axis_index("gy") * per
    gains = lax.optimization_barrier(
        gain_table.transpose(2, 0, 1, 3).reshape(blocks, rows_here * terms, observers)
    )
    sums = []
    share = observers // (shards * columns)
    for o in range(per):
        block = (first + o).astype(jnp.int32).reshape(1)
        arrived = bin_rows(block, src, arrival_bins, arrival_fracs)
        partial = jnp.einsum(
            "ct,cb->tb",
            lax.dynamic_index_in_dim(gains, first + o, 0, keepdims=False),
            arrived,
            preferred_element_type=jnp.float32,
        ).astype(jnp.bfloat16)
        parts = lax.all_to_all(partial, ("gx", "gy"), split_axis=0, concat_axis=0, tiled=True)
        sums.append(
            jnp.sum(parts.reshape(shards, columns, share, NBIN).astype(jnp.float32), axis=0)
        )
    return jnp.stack(sums, axis=1).transpose(2, 0, 1, 3).reshape(share, blocks, NBIN)


def solution(mesh):
    placed = (
        P(("gx", "gy"), None, None),
        P(("gx", "gy"), None),
        P(("gx", "gy")),
        P(("gx", "gy")),
        P("gx", None, None),
        P("gx", None, None),
        P("gx", None, None, None),
    )
    return jax.shard_map(
        on_device,
        mesh=mesh,
        in_specs=placed,
        out_specs=P(("gx", "gy"), None, None),
        check_vma=False,
    )
```

profile of v0, /device:TPU:1, one launch (start us, length us, event | category | flops | bytes accessed | tf_op | source)
XLA Modules:
  0.0 92.7 jit_solution(5781376190806400912)
XLA Ops:
  0.0 0.7 and_select_fusion.1
  0.7 0.7 fusion.22
  1.4 0.9 %broadcast_multiply_fusion = bf16[64,8,128]{2,1,0:T(8,128)(2,1)S(1)} fusion(bf16[64,8,128]{2,1,0:T(8,128)(2,1)} %param.7, bf16[64,128]{1,0:T(8,128)(2,1)S(1)} %fusion.22), kind=kLoop, calls=%fused_computation.28 | loop fusion | flops 65536 | bytes 278528 | tf_op jit(solution)/shard_map/mul | solution.py:77
  2.4 0.9 select_reduce_fusion
  3.3 0.7 multiply_add_fusion
  3.9 0.1 select_convert_fusion
  4.0 0.9 %fusion.6 = bf16[16,8,1152]{2,1,0:T(8,128)(2,1)} fusion(bf16[64,128]{1,0:T(8,128)(2,1)S(1)} %select_convert_fusion, bf16[64,1024]{1,0:T(8,128)(2,1)S(1)} %bitcast.46, s32[64]{0:T(128)S(1)} %multiply_add_fusion), kind=kOutput, calls=%fused_computation.8 | convolution fusion | flops 19324928 | bytes 442624 | tf_op jit(solution)/shard_map/dot_general | solution.py:95
  5.0 7.4 %all-to-all-start = ((bf16[16,8,1152]{2,1,0:T(8,128)(2,1)}), bf16[16,8,1152]{2,1,0:T(8,128)(2,1)S(1)}, u32[]{:S(2)}, u32[]{:S(2)}) async-start(bf16[16,8,1152]{2,1,0:T(8,128)(2,1)} %fusion.6), calls=%async_computation | async-start | bytes 589824 | tf_op jit(solution)/shard_map/all_to_all | solution.py:98
  12.4 17.0 %copy.21 = bf16[4,256,8,1024]{3,2,1,0:T(8,128)(2,1)} copy(bf16[4,256,8,1024]{3,0,2,1:T(4,128)(2,1)} %bitcast.38) | data formatting | bytes 33554432 | tf_op jit(solution)/shard_map/transpose | solution.py:112
  29.4 0.0 all-to-all-done
  29.4 2.8 %all_gather.3 = bf16[256,1152]{1,0:T(8,128)(2,1)S(1)} all-gather(bf16[128,1152]{1,0:T(8,128)(2,1)S(1)} %bitcast.43), channel_id=1, replica_groups=mesh['gx'=16,'gy'=2] {'gy'}, dimensions={0}, use_global_device_ids=true | all-gather | bytes 884736 | tf_op jit(solution)/shard_map/all_gather | solution.py:99
  32.2 0.2 fusion.18
  32.4 0.3 convolution_convert_fusion.1
  32.7 1.0 %reshape.104.src_ref = bf16[2048,128]{1,0:T(8,128)(2,1)} reshape(bf16[256,1024]{1,0:T(8,128)(2,1)S(1)} %convolution_convert_fusion.1) | data formatting | bytes 1048576 | tf_op jit(solution)/shard_map/reshape | solution.py:108
  33.8 10.9 %bin_rows.3 = bf16[2048,256]{1,0:T(8,128)(2,1)} custom-call(s32[1]{0:T(128)} %bitcast.11.block_ref, bf16[2048,128]{1,0:T(8,128)(2,1)} %reshape.104.src_ref, s32[256,4,128]{2,1,0:T(4,128)} %bins_ref.3, f32[256,4,128]{2,1,0:T(4,128)} %fracs_ref.3), custom_call_target="tpu_custom_call" | custom-call | flops 268435456 | bytes 2048000 | tf_op jit(solution)/shard_map/bin_rows/pallas_call | solution.py:51
  44.6 4.6 %fusion.10 = bf16[1024,256]{1,0:T(8,128)(2,1)} fusion(bf16[2048,256]{1,0:T(8,128)(2,1)} %bin_rows.3, bf16[4,2048,1024]{2,1,0:T(8,128)(2,1)} %bitcast.39, s32[]{:T(128)S(6)} %select_n.60), kind=kOutput, calls=%fused_computation.11 | convolution fusion | flops 1074003968 | bytes 5767172 | tf_op jit(solution)/shard_map/ct,cb->tb/dot_general | solution.py:119
  49.2 6.0 %all-to-all-start.2 = ((bf16[32,32,256]{2,1,0:T(8,128)(2,1)}), bf16[32,32,256]{2,1,0:T(8,128)(2,1)S(1)}, u32[]{:S(2)}, u32[]{:S(2)}) async-start(bf16[32,32,256]{2,1,0:T(8,128)(2,1)} %bitcast.12), calls=%async_computation.2 | async-start | bytes 1048576 | tf_op jit(solution)/shard_map/all_to_all | solution.py:125
  55.2 10.9 %bin_rows.2 = bf16[2048,256]{1,0:T(8,128)(2,1)} custom-call(s32[1]{0:T(128)} %bitcast.3.block_ref, bf16[2048,128]{1,0:T(8,128)(2,1)} %reshape.104.src_ref, s32[256,4,128]{2,1,0:T(4,128)} %bins_ref.3, f32[256,4,128]{2,1,0:T(4,128)} %fracs_ref.3), custom_call_target="tpu_custom_call" | custom-call | flops 268435456 | bytes 2048000 | tf_op jit(solution)/shard_map/bin_rows/pallas_call | solution.py:51
  66.1 4.6 %fusion.7 = bf16[1024,256]{1,0:T(8,128)(2,1)} fusion(bf16[2048,256]{1,0:T(8,128)(2,1)} %bin_rows.2, bf16[4,2048,1024]{2,1,0:T(8,128)(2,1)} %bitcast.40, s32[]{:T(128)S(6)} %select_n.51), kind=kOutput, calls=%fused_computation.10 | convolution fusion | flops 1074003968 | bytes 5767172 | tf_op jit(solution)/shard_map/ct,cb->tb/dot_general | solution.py:119
  70.7 0.0 all-to-all-done.2
  70.7 5.8 %all-to-all-start.1 = ((bf16[32,32,256]{2,1,0:T(8,128)(2,1)}), bf16[32,32,256]{2,1,0:T(8,128)(2,1)S(1)}, u32[]{:S(2)}, u32[]{:S(2)}) async-start(bf16[32,32,256]{2,1,0:T(8,128)(2,1)} %bitcast.7), calls=%async_computation.1 | async-start | bytes 1048576 | tf_op jit(solution)/shard_map/all_to_all | solution.py:125
  76.6 0.1 convert_reduce_fusion
  76.7 15.1 %all-to-all-done.1 = bf16[32,32,256]{2,1,0:T(8,128)(2,1)S(1)} async-done(((bf16[32,32,256]{2,1,0:T(8,128)(2,1)}), bf16[32,32,256]{2,1,0:T(8,128)(2,1)S(1)}, u32[]{:S(2)}, u32[]{:S(2)}) %all-to-all-start.1) | async-done | bytes 524320 | tf_op jit(solution)/shard_map/all_to_all | solution.py:125
  91.8 0.1 convert_reduce_fusion.1
  91.9 0.7 copy.17
  (6 shorter events, 0.1 us)
Async XLA Ops:
  5.0 24.4 %all-to-all-start = ((bf16[16,8,1152]{2,1,0:T(8,128)(2,1)}), bf16[16,8,1152]{2,1,0:T(8,128)(2,1)S(1)}, u32[]{:S(2)}, u32[]{:S(2)}) async-start(bf16[16,8,1152]{2,1,0:T(8,128)(2,1)} %fusion.6), calls=%async_computation | async-start | bytes 589824 | tf_op jit(solution)/shard_map/all_to_all | solution.py:98
  49.2 21.5 %all-to-all-start.2 = ((bf16[32,32,256]{2,1,0:T(8,128)(2,1)}), bf16[32,32,256]{2,1,0:T(8,128)(2,1)S(1)}, u32[]{:S(2)}, u32[]{:S(2)}) async-start(bf16[32,32,256]{2,1,0:T(8,128)(2,1)} %bitcast.12), calls=%async_computation.2 | async-start | bytes 1048576 | tf_op jit(solution)/shard_map/all_to_all | solution.py:125
  70.7 21.1 %all-to-all-start.1 = ((bf16[32,32,256]{2,1,0:T(8,128)(2,1)}), bf16[32,32,256]{2,1,0:T(8,128)(2,1)S(1)}, u32[]{:S(2)}, u32[]{:S(2)}) async-start(bf16[32,32,256]{2,1,0:T(8,128)(2,1)} %bitcast.7), calls=%async_computation.1 | async-start | bytes 1048576 | tf_op jit(solution)/shard_map/all_to_all | solution.py:125
where the time goes:
time: 93.8 us; the launch traced here: 92.7 us
  Pallas kernels  21.7 us (23%)
  starting transfers between devices  19.2 us (20%)
  local copies, waits for them, and re-layouts  18.8 us (20%)
  waiting for transfers between devices  15.1 us (16%)
  matrix products  10.4 us (11%)
  other arithmetic  4.38 us (5%)
  blocking collectives  2.8 us (3%)
    pallas_call x2, Pallas kernels, bin_rows(): pl.pallas_call(bin_kernel, out_shape=jax.ShapeDtypeStruct((rows, NBIN), j...  21.7 us
    transpose x1, local copies, waits for them, and re-layouts, on_device(): gain_table.transpose(2, 0, 1, 3)  17 us
    all_to_all x2, waiting for transfers between devices, on_device(): lax.all_to_all(partial, ('gx', 'gy'), split_axis=0, concat_axis=0, tiled=...  15.1 us
    all_to_all x2, starting transfers between devices, on_device(): lax.all_to_all(partial, ('gx', 'gy'), split_axis=0, concat_axis=0, tiled=...  11.8 us
    dot_general x2, matrix products, on_device(): jnp.einsum('ct,cb->tb', lax.dynamic_index_in_dim(gains, first + o, 0, kee...  9.21 us
    all_to_all x1, starting transfers between devices, on_device(): got = lax.all_to_all(send, 'gx', split_axis=0, concat_axis=0, tiled=True)  7.4 us
    all_gather x1, blocking collectives, on_device(): got = lax.all_gather(got, 'gy', axis=0, tiled=True)  2.8 us
  transfers between devices with their start and end apart: 3, of which 1 were waited for; matrix products, arithmetic and copies ran while one was open for 23% of the time, Pallas kernels for 12%

commit v1 on v0

v1 whole, which is shorter than its diff:
```python
import functools

import jax
import jax.numpy as jnp
from jax import lax
from jax.experimental import pallas as pl
from jax.experimental.pallas import tpu as pltpu
from jax.sharding import PartitionSpec as P

NBIN = 256
LANES = 128
LO = 64
HI = NBIN // LO
WIDE = LO + 16
CHUNK = 128
SLOTS = 4


def bf16(v):
    return v.astype(jnp.bfloat16)


def aligned(i, n):
    return pl.multiple_of(i * n, n)


def gains_kernel(per, blocks, gains_ref, out_ref, buffer, mixed, sems):
    first = lax.axis_index("gy") * per
    columns = out_ref.shape[1] // LANES
    deep = columns * blocks
    group = 256 // deep
    steps = out_ref.shape[2] // CHUNK
    size = CHUNK * deep

    def fetch(i):
        slot = lax.rem(i, SLOTS)
        return pltpu.make_async_copy(
            gains_ref.at[pl.ds(aligned(i, size), size)], buffer.at[slot], sems.at[slot]
        )

    for i in range(SLOTS - 1):
        fetch(i).start()
    height = per * columns * group
    row = lax.broadcasted_iota(jnp.int32, (height, 256), 0)
    spot = lax.broadcasted_iota(jnp.int32, (height, 256), 1)
    wanted = (
        lax.rem(row, group) * deep
        + lax.rem(row // group, columns) * blocks
        + first
        + row // (group * columns)
    )
    pick = bf16((wanted == spot).astype(jnp.float32))

    def step(i, carry):
        slot = lax.rem(i, SLOTS)

        @pl.when(i + SLOTS - 1 < steps)
        def _():
            fetch(i + SLOTS - 1).start()

        fetch(i).wait()

        def part(j, c):
            one = buffer[slot, pl.ds(aligned(j, 512), 256), :]
            two = buffer[slot, pl.ds(aligned(j, 512) + 256, 256), :]
            got = jnp.dot(
                pick, jnp.concatenate([one, two], axis=1), preferred_element_type=jnp.float32
            )
            for o in range(per):
                for t in range(columns):
                    q = (o * columns + t) * group
                    both = jnp.concatenate(
                        [got[q : q + group, :LANES], got[q : q + group, LANES:]], axis=0
                    )
                    mixed[o, pl.ds(aligned(j, 2 * group), 2 * group), t * LANES : (t + 1) * LANES] = bf16(both)
            return c

        lax.fori_loop(0, CHUNK // (2 * group), part, 0, unroll=True)
        for o in range(per):
            for t in range(columns):
                out_ref[o, t * LANES : (t + 1) * LANES, pl.ds(aligned(i, CHUNK), CHUNK)] = mixed[
                    o, :, t * LANES : (t + 1) * LANES
                ].T
        return carry

    lax.fori_loop(0, steps, step, 0)


def turned_gains(per, gain_table):
    rows, terms, blocks, observers = gain_table.shape
    columns = observers // LANES
    flat = (
        gain_table.reshape(rows * terms, blocks, columns, LANES)
        .transpose(0, 2, 1, 3)
        .reshape(-1, LANES)
    )
    return pl.pallas_call(
        functools.partial(gains_kernel, per, blocks),
        out_shape=jax.ShapeDtypeStruct((per, observers, rows * terms), jnp.bfloat16),
        in_specs=[pl.BlockSpec(memory_space=pl.ANY)],
        out_specs=pl.BlockSpec(memory_space=pltpu.VMEM),
        scratch_shapes=[
            pltpu.VMEM((SLOTS, CHUNK * columns * blocks, LANES), jnp.bfloat16),
            pltpu.VMEM((per, CHUNK, observers), jnp.bfloat16),
            pltpu.SemaphoreType.DMA((SLOTS,)),
        ],
        name="turned_gains",
        cost_estimate=pl.CostEstimate(
            flops=4 * 10**9, bytes_accessed=2 * gain_table.size * 2, transcendentals=0
        ),
    )(flat)


def spread_kernel(order, src_ref, bins_ref, fracs_ref, gains_ref, out_ref, table, arrived):
    block = lax.axis_index("gy") * gains_ref.shape[0] + order
    rows = bins_ref.shape[0]
    bins = bins_ref[:, pl.ds(block, 1), :].reshape(rows, LANES)
    fracs = fracs_ref[:, pl.ds(block, 1), :].reshape(rows, LANES)
    table[0] = (bins // LO).astype(jnp.float32)
    table[1] = lax.rem(bins, LO).astype(jnp.float32)
    table[2] = 1.0 - fracs
    table[3] = fracs
    spots = bf16(lax.broadcasted_iota(jnp.int32, (WIDE, LANES), 0).astype(jnp.float32))
    lane = lax.broadcasted_iota(jnp.int32, (16, LANES), 1)
    upper = lax.broadcasted_iota(jnp.int32, (16, LANES), 0) < 8
    zero = jnp.zeros((), jnp.bfloat16)

    def spread(kind, row, n):
        return jnp.broadcast_to(table[kind, pl.ds(row, 1), :], (n, LANES))

    def weights_of(row):
        low = spread(1, row, WIDE)
        return jnp.where(
            spots == bf16(low),
            bf16(spread(2, row, WIDE)),
            jnp.where(spots == bf16(low + 1.0), bf16(spread(3, row, WIDE)), zero),
        )

    def pair(i, carry):
        both = src_ref[pl.ds(aligned(i, 16), 16), :]
        left = bf16(jnp.where(upper, spread(0, 2 * i, 16), -1.0))
        right = bf16(jnp.where(upper, -1.0, spread(0, 2 * i + 1, 16)))
        lhs = []
        for h in range(HI):
            at = jnp.asarray(h, jnp.bfloat16)
            lhs.append(
                jnp.concatenate(
                    [jnp.where(left == at, both, zero), jnp.where(right == at, both, zero)], axis=1
                )
            )
        rhs = jnp.concatenate([weights_of(2 * i), weights_of(2 * i + 1)], axis=1)
        got = lax.dot_general(
            jnp.concatenate(lhs, axis=0), rhs, (((1,), (1,)), ((), ())), preferred_element_type=jnp.float32
        )
        got = jnp.concatenate([got, jnp.zeros((16 * HI, LANES - WIDE), jnp.float32)], axis=1)
        tiles = []
        carried = None
        for t in range(NBIN // LANES):
            even = got[32 * t : 32 * t + 16, :]
            odd = pltpu.roll(got[32 * t + 16 : 32 * t + 32, :], LO, 1)
            tile = even + jnp.where(lane >= LO, odd, 0.0)
            if carried is not None:
                tile = tile + jnp.where(lane < LO, carried, 0.0)
            carried = odd
            tiles.append(tile)
        arrived[pl.ds(aligned(i, 16), 16), :] = bf16(jnp.concatenate(tiles, axis=1))
        return carry

    lax.fori_loop(0, rows // 2, pair, 0, unroll=16)
    tall = 256

    def strip(i, carry):
        out_ref[pl.ds(aligned(i, tall), tall), :] = bf16(
            jnp.dot(
                gains_ref[order, pl.ds(aligned(i, tall), tall), :], arrived[...], preferred_element_type=jnp.float32
            )
        )
        return carry

    lax.fori_loop(0, out_ref.shape[0] // tall, strip, 0)


def partial_signals(order, src, bins, fracs, gains):
    observers = gains.shape[1]
    rows = src.shape[0]
    return pl.pallas_call(
        functools.partial(spread_kernel, order),
        out_shape=jax.ShapeDtypeStruct((observers, NBIN), jnp.bfloat16),
        in_specs=[pl.BlockSpec(memory_space=pltpu.VMEM)] * 4,
        out_specs=pl.BlockSpec(memory_space=pltpu.VMEM),
        scratch_shapes=[
            pltpu.VMEM((4, bins.shape[0], LANES), jnp.float32),
            pltpu.VMEM((rows, NBIN), jnp.bfloat16),
        ],
        name="partial_signals",
        cost_estimate=pl.CostEstimate(
            flops=4 * rows * observers * NBIN, bytes_accessed=8 * 10**6, transcendentals=0
        ),
    )(src, bins, fracs, gains)


def on_device(sources, owners, strip_rows, panel_counts, arrival_bins, arrival_fracs, gain_table):
    strip_count, terms, panels = sources.shape
    shards = lax.axis_size("gx")
    columns = lax.axis_size("gy")
    capacity = 2 * strip_count // shards
    blocks = arrival_bins.shape[1]
    observers = gain_table.shape[3]
    rows_here = arrival_bins.shape[0]
    live_mask = (jnp.arange(panels, dtype=jnp.int32)[None, :] < panel_counts[:, None]).astype(
        jnp.bfloat16
    )
    masked = (sources * live_mask[:, None, :]).reshape(strip_count, terms * panels)
    lane = jnp.arange(128, dtype=jnp.int32)[None, :]
    coded = jnp.where(
        lane == 0,
        (strip_rows // 128)[:, None],
        jnp.where(lane == 1, (strip_rows % 128)[:, None], jnp.where(lane == 2, 1, 0)),
    ).astype(jnp.bfloat16)
    payload = jnp.concatenate([masked, coded], axis=1)
    targets = owners[:, 0]
    earlier = (
        jnp.arange(strip_count, dtype=jnp.int32)[None, :]
        < jnp.arange(strip_count, dtype=jnp.int32)[:, None]
    )
    order_in = jnp.sum(
        jnp.where(earlier & (targets[None, :] == targets[:, None]), 1, 0).astype(jnp.int32), axis=1
    )
    slot_of = targets * capacity + order_in
    placing = jnp.arange(shards * capacity, dtype=jnp.int32)[:, None] == slot_of[None, :]
    send = jnp.dot(
        placing.astype(jnp.bfloat16), payload, preferred_element_type=jnp.float32
    ).astype(jnp.bfloat16)
    got = lax.all_to_all(send, "gx", split_axis=0, concat_axis=0, tiled=True)
    got = lax.all_gather(got, "gy", axis=0, tiled=True)
    codes = got[:, terms * panels :].astype(jnp.int32)
    got_rows = jnp.where(codes[:, 2] > 0, codes[:, 0] * 128 + codes[:, 1], -1)
    row_hot = (jnp.arange(rows_here, dtype=jnp.int32)[:, None] == got_rows[None, :]).astype(
        jnp.bfloat16
    )
    row_sources = jnp.dot(
        row_hot, got[:, : terms * panels], preferred_element_type=jnp.float32
    ).astype(jnp.bfloat16)
    src = row_sources.reshape(rows_here * terms, panels)
    per = blocks // columns
    gains = turned_gains(per, gain_table)
    sums = []
    share = observers // (shards * columns)
    for o in range(per):
        partial = partial_signals(o, src, arrival_bins, arrival_fracs, gains)
        parts = lax.all_to_all(partial, ("gx", "gy"), split_axis=0, concat_axis=0, tiled=True)
        sums.append(
            jnp.sum(parts.reshape(shards, columns, share, NBIN).astype(jnp.float32), axis=0)
        )
    return jnp.stack(sums, axis=1).transpose(2, 0, 1, 3).reshape(share, blocks, NBIN)


def solution(mesh):
    placed = (
        P(("gx", "gy"), None, None),
        P(("gx", "gy"), None),
        P(("gx", "gy")),
        P(("gx", "gy")),
        P("gx", None, None),
        P("gx", None, None),
        P("gx", None, None, None),
    )
    return jax.shard_map(
        on_device,
        mesh=mesh,
        in_specs=placed,
        out_specs=P(("gx", "gy"), None, None),
        check_vma=False,
    )
```

time: 93.8 us -> 81.9 us (0.87)
  local copies, waits for them, and re-layouts: 18.8 us -> 1.84 us
  Pallas kernels: 21.7 us -> 34.1 us
  matrix products: 10.4 us -> 1.27 us
  waiting for transfers between devices: 15.1 us -> 19.5 us
  starting transfers between devices: 19.2 us -> 16.8 us
    transpose x1 -> x0, local copies, waits for them, and re-layouts: 17 us -> none  [on_device(): gain_table.transpose(2, 0, 1, 3)]
    pallas_call x2 -> x3, Pallas kernels: 21.7 us -> 34.1 us  [the longest x2 21.8 us: partial_signals(): pl.pallas_call(functools.partial(spread_kernel, order), out_shape=jax.Sha...]
    dot_general x2 -> x0, matrix products: 9.21 us -> none  [on_device(): jnp.einsum('ct,cb->tb', lax.dynamic_index_in_dim(gains, first + o, 0, kee...]
    all_to_all x2, waiting for transfers between devices: 15.1 us -> 19.5 us  [on_device(): lax.all_to_all(partial, ('gx', 'gy'), split_axis=0, concat_axis=0, tiled=...]
    all_to_all x2, starting transfers between devices: 11.8 us -> 9.39 us  [on_device(): lax.all_to_all(partial, ('gx', 'gy'), split_axis=0, concat_axis=0, tiled=...]
  transfers between devices with their start and end apart: 3 -> 3, of which waited for: 1 -> 2; matrix products, arithmetic and copies ran while one was open for 23% -> 0% of each run, Pallas kernels for 12% -> 29%
where the time goes in v1:
time: 81.9 us; the launch traced here: 80.8 us
  Pallas kernels  34.1 us (42%)
  waiting for transfers between devices  19.5 us (24%)
  starting transfers between devices  16.8 us (21%)
  other arithmetic  4.38 us (5%)
  blocking collectives  2.8 us (3%)
  local copies, waits for them, and re-layouts  1.84 us (2%)
  matrix products  1.27 us (2%)
    pallas_call x2, Pallas kernels, partial_signals(): pl.pallas_call(functools.partial(spread_kernel, order), out_shape=jax.Sha...  21.8 us
    all_to_all x2, waiting for transfers between devices, on_device(): lax.all_to_all(partial, ('gx', 'gy'), split_axis=0, concat_axis=0, tiled=...  19.5 us
    pallas_call x1, Pallas kernels, turned_gains(): pl.pallas_call(functools.partial(gains_kernel, per, blocks), out_shape=ja...  12.3 us
    all_to_all x2, starting transfers between devices, on_device(): lax.all_to_all(partial, ('gx', 'gy'), split_axis=0, concat_axis=0, tiled=...  9.39 us
    all_to_all x1, starting transfers between devices, on_device(): got = lax.all_to_all(send, 'gx', split_axis=0, concat_axis=0, tiled=True)  7.41 us
    all_gather x1, blocking collectives, on_device(): got = lax.all_gather(got, 'gy', axis=0, tiled=True)  2.8 us
  transfers between devices with their start and end apart: 3, of which 2 were waited for; matrix products, arithmetic and copies ran while one was open for 0% of the time, Pallas kernels for 29%

profile of v1, /device:TPU:1, one launch (start us, length us, event | category | flops | bytes accessed | tf_op | source)
XLA Modules:
  0.0 80.8 jit_solution(9259042570882102814)
XLA Ops:
  0.0 0.9 %select_reduce_fusion = s32[64]{0:T(128)S(1)} fusion(s32[64]{0:T(128)} %bitcast.36), kind=kLoop, calls=%fused_computation.24 | loop fusion | flops 20416 | bytes 512 | tf_op jit(solution)/shard_map/reduce_sum | solution.py:226
  0.9 0.7 multiply_add_fusion
  1.6 0.7 and_select_fusion.1
  2.3 0.7 fusion.10
  3.0 0.9 %broadcast_multiply_fusion = bf16[64,8,128]{2,1,0:T(8,128)(2,1)S(1)} fusion(bf16[64,8,128]{2,1,0:T(8,128)(2,1)} %param.7, bf16[64,128]{1,0:T(8,128)(2,1)S(1)} %fusion.10), kind=kLoop, calls=%fused_computation.19 | loop fusion | flops 65536 | bytes 278528 | tf_op jit(solution)/shard_map/mul | solution.py:213
  3.9 0.1 select_convert_fusion
  4.0 1.0 %fusion = bf16[16,8,1152]{2,1,0:T(8,128)(2,1)} fusion(bf16[64,128]{1,0:T(8,128)(2,1)S(1)} %select_convert_fusion, bf16[64,1024]{1,0:T(8,128)(2,1)S(1)} %bitcast.33, s32[64]{0:T(128)S(1)} %multiply_add_fusion), kind=kOutput, calls=%fused_computation.1 | convolution fusion | flops 19324928 | bytes 442624 | tf_op jit(solution)/shard_map/dot_general | solution.py:231
  5.0 7.4 %all-to-all-start = ((bf16[16,8,1152]{2,1,0:T(8,128)(2,1)}), bf16[16,8,1152]{2,1,0:T(8,128)(2,1)S(1)}, u32[]{:S(2)}, u32[]{:S(2)}) async-start(bf16[16,8,1152]{2,1,0:T(8,128)(2,1)} %fusion), calls=%async_computation | async-start | bytes 589824 | tf_op jit(solution)/shard_map/all_to_all | solution.py:234
  12.4 12.3 %turned_gains.1.gains_ref = bf16[2,1024,2048]{2,1,0:T(8,128)(2,1)} custom-call(bf16[65536,128]{1,0:T(8,128)(2,1)} %bitcast.25), custom_call_target="tpu_custom_call" | custom-call | flops 4000000000 | bytes 33554432 | tf_op jit(solution)/shard_map/turned_gains/pallas_call | solution.py:97
  24.7 0.0 all-to-all-done
  24.7 2.8 %all_gather.3 = bf16[256,1152]{1,0:T(8,128)(2,1)S(1)} all-gather(bf16[128,1152]{1,0:T(8,128)(2,1)S(1)} %bitcast.30), channel_id=1, replica_groups=mesh['gx'=16,'gy'=2] {'gy'}, dimensions={0}, use_global_device_ids=true | all-gather | bytes 884736 | tf_op jit(solution)/shard_map/all_gather | solution.py:235
  27.6 0.2 fusion.6
  27.8 0.3 convolution_convert_fusion.1
  28.1 1.1 %reshape.99.src_ref = bf16[2048,128]{1,0:T(8,128)(2,1)} reshape(bf16[256,1024]{1,0:T(8,128)(2,1)S(1)} %convolution_convert_fusion.1) | data formatting | bytes 1048576 | tf_op jit(solution)/shard_map/reshape | solution.py:244
  29.2 11.0 %partial_signals.3 = bf16[1024,256]{1,0:T(8,128)(2,1)} custom-call(bf16[2048,128]{1,0:T(8,128)(2,1)} %reshape.99.src_ref, s32[256,4,128]{2,1,0:T(4,128)} %bins_ref.3, f32[256,4,128]{2,1,0:T(4,128)} %fracs_ref.3, bf16[2,1024,2048]{2,1,0:T(8,128)(2,1)} %turned_gains.1.gains_ref), custom_call_target="tpu_custom_call" | custom-call | flops 2147483648 | bytes 8000000 | tf_op jit(solution)/shard_map/partial_signals/pallas_call | solution.py:186
  40.1 6.0 %all-to-all-start.2 = ((bf16[32,32,256]{2,1,0:T(8,128)(2,1)}), bf16[32,32,256]{2,1,0:T(8,128)(2,1)S(1)}, u32[]{:S(2)}, u32[]{:S(2)}) async-start(bf16[32,32,256]{2,1,0:T(8,128)(2,1)} %bitcast.27), calls=%async_computation.2 | async-start | bytes 1048576 | tf_op jit(solution)/shard_map/all_to_all | solution.py:251
  46.2 10.8 %partial_signals.2 = bf16[1024,256]{1,0:T(8,128)(2,1)} custom-call(bf16[2048,128]{1,0:T(8,128)(2,1)} %reshape.99.src_ref, s32[256,4,128]{2,1,0:T(4,128)} %bins_ref.3, f32[256,4,128]{2,1,0:T(4,128)} %fracs_ref.3, bf16[2,1024,2048]{2,1,0:T(8,128)(2,1)} %turned_gains.1.gains_ref), custom_call_target="tpu_custom_call" | custom-call | flops 2147483648 | bytes 8000000 | tf_op jit(solution)/shard_map/partial_signals/pallas_call | solution.py:186
  57.0 4.4 %all-to-all-done.2 = bf16[32,32,256]{2,1,0:T(8,128)(2,1)S(1)} async-done(((bf16[32,32,256]{2,1,0:T(8,128)(2,1)}), bf16[32,32,256]{2,1,0:T(8,128)(2,1)S(1)}, u32[]{:S(2)}, u32[]{:S(2)}) %all-to-all-start.2) | async-done | bytes 524320 | tf_op jit(solution)/shard_map/all_to_all | solution.py:251
  61.4 3.4 %all-to-all-start.1 = ((bf16[32,32,256]{2,1,0:T(8,128)(2,1)}), bf16[32,32,256]{2,1,0:T(8,128)(2,1)S(1)}, u32[]{:S(2)}, u32[]{:S(2)}) async-start(bf16[32,32,256]{2,1,0:T(8,128)(2,1)} %bitcast.26), calls=%async_computation.1 | async-start | bytes 1048576 | tf_op jit(solution)/shard_map/all_to_all | solution.py:251
  64.8 0.1 convert_reduce_fusion
  64.8 15.1 %all-to-all-done.1 = bf16[32,32,256]{2,1,0:T(8,128)(2,1)S(1)} async-done(((bf16[32,32,256]{2,1,0:T(8,128)(2,1)}), bf16[32,32,256]{2,1,0:T(8,128)(2,1)S(1)}, u32[]{:S(2)}, u32[]{:S(2)}) %all-to-all-start.1) | async-done | bytes 524320 | tf_op jit(solution)/shard_map/all_to_all | solution.py:251
  80.0 0.1 convert_reduce_fusion.1
  80.1 0.7 copy.18
  (6 shorter events, 0.1 us)
Async XLA Ops:
  5.0 19.7 %all-to-all-start = ((bf16[16,8,1152]{2,1,0:T(8,128)(2,1)}), bf16[16,8,1152]{2,1,0:T(8,128)(2,1)S(1)}, u32[]{:S(2)}, u32[]{:S(2)}) async-start(bf16[16,8,1152]{2,1,0:T(8,128)(2,1)} %fusion), calls=%async_computation | async-start | bytes 589824 | tf_op jit(solution)/shard_map/all_to_all | solution.py:234
  40.1 21.3 %all-to-all-start.2 = ((bf16[32,32,256]{2,1,0:T(8,128)(2,1)}), bf16[32,32,256]{2,1,0:T(8,128)(2,1)S(1)}, u32[]{:S(2)}, u32[]{:S(2)}) async-start(bf16[32,32,256]{2,1,0:T(8,128)(2,1)} %bitcast.27), calls=%async_computation.2 | async-start | bytes 1048576 | tf_op jit(solution)/shard_map/all_to_all | solution.py:251
  61.4 18.6 %all-to-all-start.1 = ((bf16[32,32,256]{2,1,0:T(8,128)(2,1)}), bf16[32,32,256]{2,1,0:T(8,128)(2,1)S(1)}, u32[]{:S(2)}, u32[]{:S(2)}) async-start(bf16[32,32,256]{2,1,0:T(8,128)(2,1)} %bitcast.26), calls=%async_computation.1 | async-start | bytes 1048576 | tf_op jit(solution)/shard_map/all_to_all | solution.py:251

commit v2 on v1

--- a/solution.py
+++ b/solution.py
@@ -14,6 +14,8 @@
 WIDE = LO + 16
 CHUNK = 128
 SLOTS = 4
+UNROLL = 16
+MESH = pl.DeviceIdType.MESH
 
 
 def bf16(v):
@@ -111,91 +113,255 @@
     )(flat)
 
 
-def spread_kernel(order, src_ref, bins_ref, fracs_ref, gains_ref, out_ref, table, arrived):
-    block = lax.axis_index("gy") * gains_ref.shape[0] + order
+def spread_kernel(
+    per, share, src_ref, bins_ref, fracs_ref, gains_hbm, out_ref,
+    gains, table, arrived, first_out, first_in, kept, last, second_out, second_in, third_out, third_in,
+    gain_sems, one_send, one_recv, two_send, two_recv, three_send, three_recv,
+):
+    g = lax.axis_index("gx")
+    q = lax.axis_index("gy")
+    shards = lax.axis_size("gx")
+    columns = lax.axis_size("gy")
+    depth = shards // 4
+    bit0, bit1, z = lax.rem(g, 2), lax.rem(g // 2, 2), g // 4
+    flips = (g + 1 - 2 * bit0, g + 2 - 4 * bit1)
+    corner = lax.rem(g, 4)
     rows = bins_ref.shape[0]
-    bins = bins_ref[:, pl.ds(block, 1), :].reshape(rows, LANES)
-    fracs = fracs_ref[:, pl.ds(block, 1), :].reshape(rows, LANES)
-    table[0] = (bins // LO).astype(jnp.float32)
-    table[1] = lax.rem(bins, LO).astype(jnp.float32)
-    table[2] = 1.0 - fracs
-    table[3] = fracs
+    wide = columns * share
+    tall = depth * wide
+    half = NBIN // 2
+
+    def fetch(j):
+        return pltpu.make_async_copy(gains_hbm.at[j], gains.at[j], gain_sems.at[j])
+
+    for j in range(per):
+        fetch(j).start()
+
+    barrier = pltpu.get_barrier_semaphore()
+
+    def greet(to_g, to_q):
+        pl.semaphore_signal(barrier, inc=1, device_id=(to_g, to_q), device_id_type=MESH)
+
+    for partner in flips:
+        greet(partner, q)
+
+    def others(body):
+        def one(i, c):
+            to_z, to_q = i // columns, lax.rem(i, columns)
+
+            @pl.when(jnp.logical_or(to_z != z, to_q != q))
+            def _():
+                body(i, to_z, to_q)
+
+            return c
+
+        lax.fori_loop(0, depth * columns, one, 0)
+
+    others(lambda i, to_z, to_q: greet(to_z * 4 + corner, to_q))
+
     spots = bf16(lax.broadcasted_iota(jnp.int32, (WIDE, LANES), 0).astype(jnp.float32))
     lane = lax.broadcasted_iota(jnp.int32, (16, LANES), 1)
     upper = lax.broadcasted_iota(jnp.int32, (16, LANES), 0) < 8
     zero = jnp.zeros((), jnp.bfloat16)
 
-    def spread(kind, row, n):
-        return jnp.broadcast_to(table[kind, pl.ds(row, 1), :], (n, LANES))
-
-    def weights_of(row):
-        low = spread(1, row, WIDE)
-        return jnp.where(
-            spots == bf16(low),
-            bf16(spread(2, row, WIDE)),
-            jnp.where(spots == bf16(low + 1.0), bf16(spread(3, row, WIDE)), zero),
-        )
-
-    def pair(i, carry):
-        both = src_ref[pl.ds(aligned(i, 16), 16), :]
-        left = bf16(jnp.where(upper, spread(0, 2 * i, 16), -1.0))
-        right = bf16(jnp.where(upper, -1.0, spread(0, 2 * i + 1, 16)))
-        lhs = []
-        for h in range(HI):
-            at = jnp.asarray(h, jnp.bfloat16)
-            lhs.append(
-                jnp.concatenate(
-                    [jnp.where(left == at, both, zero), jnp.where(right == at, both, zero)], axis=1
+    def prepare(j):
+        block = q * per + j
+        bins = bins_ref[:, pl.ds(block, 1), :].reshape(rows, LANES)
+        fracs = fracs_ref[:, pl.ds(block, 1), :].reshape(rows, LANES)
+        table[j, 0] = (bins // LO).astype(jnp.float32)
+        table[j, 1] = lax.rem(bins, LO).astype(jnp.float32)
+        table[j, 2] = 1.0 - fracs
+        table[j, 3] = fracs
+
+    def scatter(j):
+        def spread(kind, row, n):
+            return jnp.broadcast_to(table[j, kind, pl.ds(row, 1), :], (n, LANES))
+
+        def weights_of(row):
+            low = spread(1, row, WIDE)
+            return jnp.where(
+                spots == bf16(low),
+                bf16(spread(2, row, WIDE)),
+                jnp.where(spots == bf16(low + 1.0), bf16(spread(3, row, WIDE)), zero),
+            )
+
+        def pair(i, carry):
+            both = src_ref[pl.ds(aligned(i, 16), 16), :]
+            left = bf16(jnp.where(upper, spread(0, 2 * i, 16), -1.0))
+            right = bf16(jnp.where(upper, -1.0, spread(0, 2 * i + 1, 16)))
+            lhs = []
+            for h in range(HI):
+                at = jnp.asarray(h, jnp.bfloat16)
+                lhs.append(
+                    jnp.concatenate(
+                        [jnp.where(left == at, both, zero), jnp.where(right == at, both, zero)], axis=1
+                    )
                 )
+            rhs = jnp.concatenate([weights_of(2 * i), weights_of(2 * i + 1)], axis=1)
+            got = lax.dot_general(
+                jnp.concatenate(lhs, axis=0), rhs, (((1,), (1,)), ((), ())), preferred_element_type=jnp.float32
             )
-        rhs = jnp.concatenate([weights_of(2 * i), weights_of(2 * i + 1)], axis=1)
-        got = lax.dot_general(
-            jnp.concatenate(lhs, axis=0), rhs, (((1,), (1,)), ((), ())), preferred_element_type=jnp.float32
-        )
-        got = jnp.concatenate([got, jnp.zeros((16 * HI, LANES - WIDE), jnp.float32)], axis=1)
-        tiles = []
-        carried = None
-        for t in range(NBIN // LANES):
-            even = got[32 * t : 32 * t + 16, :]
-            odd = pltpu.roll(got[32 * t + 16 : 32 * t + 32, :], LO, 1)
-            tile = even + jnp.where(lane >= LO, odd, 0.0)
-            if carried is not None:
-                tile = tile + jnp.where(lane < LO, carried, 0.0)
-            carried = odd
-            tiles.append(tile)
-        arrived[pl.ds(aligned(i, 16), 16), :] = bf16(jnp.concatenate(tiles, axis=1))
-        return carry
-
-    lax.fori_loop(0, rows // 2, pair, 0, unroll=16)
-    tall = 256
-
-    def strip(i, carry):
-        out_ref[pl.ds(aligned(i, tall), tall), :] = bf16(
-            jnp.dot(
-                gains_ref[order, pl.ds(aligned(i, tall), tall), :], arrived[...], preferred_element_type=jnp.float32
+            got = jnp.concatenate([got, jnp.zeros((16 * HI, LANES - WIDE), jnp.float32)], axis=1)
+            tiles = []
+            carried = None
+            for t in range(NBIN // LANES):
+                even = got[32 * t : 32 * t + 16, :]
+                odd = pltpu.roll(got[32 * t + 16 : 32 * t + 32, :], LO, 1)
+                tile = even + jnp.where(lane >= LO, odd, 0.0)
+                if carried is not None:
+                    tile = tile + jnp.where(lane < LO, carried, 0.0)
+                carried = odd
+                tiles.append(tile)
+            arrived[pl.ds(aligned(i, 16), 16), :] = bf16(jnp.concatenate(tiles, axis=1))
+            return carry
+
+        lax.fori_loop(0, rows // 2, pair, 0, unroll=UNROLL)
+
+    def multiply(j, c0, c1):
+        lhs = jnp.concatenate(
+            [
+                gains[j, pl.ds(pl.multiple_of((k * 4 + c1 * 2 + c0) * wide, 8), wide), :]
+                for k in range(depth)
+            ],
+            axis=0,
+        )
+        return jnp.dot(lhs, arrived[...], preferred_element_type=jnp.float32)
+
+    def stage_one(j, h, part):
+        return pltpu.make_async_remote_copy(
+            src_ref=first_out.at[j, h, part],
+            dst_ref=first_in.at[j, h, part],
+            send_sem=one_send.at[j, h, part],
+            recv_sem=one_recv.at[j, h, part],
+            device_id=(flips[h], q),
+            device_id_type=MESH,
+        )
+
+    def stage_two(j, h):
+        return pltpu.make_async_remote_copy(
+            src_ref=second_out.at[j, h],
+            dst_ref=second_in.at[j, h],
+            send_sem=two_send.at[j, h],
+            recv_sem=two_recv.at[j, h],
+            device_id=(flips[1 - h], q),
+            device_id_type=MESH,
+        )
+
+    def stage_three(j, i, to_z, to_q):
+        return pltpu.make_async_remote_copy(
+            src_ref=third_out.at[j, i],
+            dst_ref=third_in.at[j, z * columns + q],
+            send_sem=three_send.at[j, i],
+            recv_sem=three_recv.at[j, z * columns + q],
+            device_id=(to_z * 4 + corner, to_q),
+            device_id_type=MESH,
+        )
+
+    def arrival(j, i):
+        return pltpu.make_async_remote_copy(
+            src_ref=third_out.at[j, i],
+            dst_ref=third_in.at[j, i],
+            send_sem=three_send.at[j, i],
+            recv_sem=three_recv.at[j, i],
+            device_id=((i // columns) * 4 + corner, lax.rem(i, columns)),
+            device_id_type=MESH,
+        )
+
+    sides = (slice(0, half), slice(half, NBIN))
+
+    def products(j):
+        got = multiply(j, 1 - bit0, 1 - bit1)
+        for h in range(2):
+            first_out[j, h, 0] = bf16(got[:, sides[h]])
+            stage_one(j, h, 0).start()
+        got = multiply(j, 1 - bit0, bit1)
+        first_out[j, 0, 1] = bf16(got[:, sides[0]])
+        stage_one(j, 0, 1).start()
+        kept[j, 1] = got[:, sides[1]]
+        got = multiply(j, bit0, 1 - bit1)
+        first_out[j, 1, 1] = bf16(got[:, sides[1]])
+        stage_one(j, 1, 1).start()
+        kept[j, 0] = got[:, sides[0]]
+        got = multiply(j, bit0, bit1)
+        for h in range(2):
+            last[j, h] = got[:, sides[h]]
+
+    for j in range(per):
+        prepare(j)
+    for j in range(per):
+        scatter(j)
+        fetch(j).wait()
+        if j == 0:
+            pl.semaphore_wait(barrier, 1 + depth * columns)
+        products(j)
+    for j in range(per):
+        for h in range(2):
+            stage_one(j, h, 0).wait_recv()
+            second_out[j, h] = bf16(kept[j, h] + first_in[j, h, 0].astype(jnp.float32))
+            stage_two(j, h).start()
+    for j in range(per):
+        for h in range(2):
+            stage_one(j, h, 1).wait_recv()
+            stage_two(j, h).wait_recv()
+            total = (
+                last[j, h]
+                + first_in[j, h, 1].astype(jnp.float32)
+                + second_in[j, h].astype(jnp.float32)
             )
-        )
-        return carry
-
-    lax.fori_loop(0, out_ref.shape[0] // tall, strip, 0)
-
-
-def partial_signals(order, src, bins, fracs, gains):
+            third_out[j, :, :, sides[h]] = bf16(total).reshape(depth * columns, share, half)
+        others(lambda i, to_z, to_q: stage_three(j, i, to_z, to_q).start())
+        third_in[j, z * columns + q] = third_out[j, z * columns + q]
+    for j in range(per):
+        others(lambda i, to_z, to_q: arrival(j, i).wait_recv())
+        for c in range(columns):
+            total = third_in[j, c].astype(jnp.float32)
+            for k in range(1, depth):
+                total = total + third_in[j, k * columns + c].astype(jnp.float32)
+            out_ref[c * per + j] = total
+    for j in range(per):
+        for h in range(2):
+            for part in range(2):
+                stage_one(j, h, part).wait_send()
+            stage_two(j, h).wait_send()
+        others(lambda i, to_z, to_q: stage_three(j, i, to_z, to_q).wait_send())
+
+
+def summed_signals(per, src, bins, fracs, gains):
     observers = gains.shape[1]
     rows = src.shape[0]
+    shards, columns = lax.axis_size("gx"), lax.axis_size("gy")
+    share = observers // (shards * columns)
+    peers = shards // 4 * columns
+    tall = peers * share
+    half = NBIN // 2
+    dma = pltpu.SemaphoreType.DMA
     return pl.pallas_call(
-        functools.partial(spread_kernel, order),
-        out_shape=jax.ShapeDtypeStruct((observers, NBIN), jnp.bfloat16),
-        in_specs=[pl.BlockSpec(memory_space=pltpu.VMEM)] * 4,
+        functools.partial(spread_kernel, per, share),
+        out_shape=jax.ShapeDtypeStruct((per * columns, share, NBIN), jnp.float32),
+        in_specs=[pl.BlockSpec(memory_space=pltpu.VMEM)] * 3 + [pl.BlockSpec(memory_space=pl.ANY)],
         out_specs=pl.BlockSpec(memory_space=pltpu.VMEM),
         scratch_shapes=[
-            pltpu.VMEM((4, bins.shape[0], LANES), jnp.float32),
+            pltpu.VMEM((per, observers, rows), jnp.bfloat16),
+            pltpu.VMEM((per, 4, bins.shape[0], LANES), jnp.float32),
             pltpu.VMEM((rows, NBIN), jnp.bfloat16),
+            pltpu.VMEM((per, 2, 2, tall, half), jnp.bfloat16),
+            pltpu.VMEM((per, 2, 2, tall, half), jnp.bfloat16),
+            pltpu.VMEM((per, 2, tall, half), jnp.float32),
+            pltpu.VMEM((per, 2, tall, half), jnp.float32),
+            pltpu.VMEM((per, 2, tall, half), jnp.bfloat16),
+            pltpu.VMEM((per, 2, tall, half), jnp.bfloat16),
+            pltpu.VMEM((per, peers, share, NBIN), jnp.bfloat16),
+            pltpu.VMEM((per, peers, share, NBIN), jnp.bfloat16),
+            dma((per,)),
+            dma((per, 2, 2)),
+            dma((per, 2, 2)),
+            dma((per, 2)),
+            dma((per, 2)),
+            dma((per, peers)),
+            dma((per, peers)),
         ],
-        name="partial_signals",
-        cost_estimate=pl.CostEstimate(
-            flops=4 * rows * observers * NBIN, bytes_accessed=8 * 10**6, transcendentals=0
-        ),
+        compiler_params=pltpu.CompilerParams(collective_id=0, has_side_effects=True),
+        name="summed_signals",
     )(src, bins, fracs, gains)
 
 
@@ -244,15 +410,7 @@
     src = row_sources.reshape(rows_here * terms, panels)
     per = blocks // columns
     gains = turned_gains(per, gain_table)
-    sums = []
-    share = observers // (shards * columns)
-    for o in range(per):
-        partial = partial_signals(o, src, arrival_bins, arrival_fracs, gains)
-        parts = lax.all_to_all(partial, ("gx", "gy"), split_axis=0, concat_axis=0, tiled=True)
-        sums.append(
-            jnp.sum(parts.reshape(shards, columns, share, NBIN).astype(jnp.float32), axis=0)
-        )
-    return jnp.stack(sums, axis=1).transpose(2, 0, 1, 3).reshape(share, blocks, NBIN)
+    return summed_signals(per, src, arrival_bins, arrival_fracs, gains).transpose(1, 0, 2)
 
 
 def solution(mesh):

time: 81.9 us -> 61.9 us (0.76)
  waiting for transfers between devices: 19.5 us -> 0.01 us
  starting transfers between devices: 16.8 us -> 7.41 us
  Pallas kernels: 34.1 us -> 42.7 us
  local copies, waits for them, and re-layouts: 1.84 us -> 2.74 us
    all_to_all x2 -> x0, waiting for transfers between devices: 19.5 us -> none  [on_device(): lax.all_to_all(partial, ('gx', 'gy'), split_axis=0, concat_axis=0, tiled=...]
    all_to_all x2 -> x0, starting transfers between devices: 9.39 us -> none  [on_device(): lax.all_to_all(partial, ('gx', 'gy'), split_axis=0, concat_axis=0, tiled=...]
    pallas_call x2 -> x1, Pallas kernels: 21.8 us -> 30.4 us  [summed_signals(): pl.pallas_call(functools.partial(spread_kernel, per, share), out_shape=ja...]
    transpose x1, local copies, waits for them, and re-layouts: 0.01 us -> 1.65 us  [on_device(): summed_signals(per, src, arrival_bins, arrival_fracs, gains)]
  transfers between devices with their start and end apart: 3 -> 1, of which waited for: 2 -> 0; matrix products, arithmetic and copies ran while one was open for 0% -> 0% of each run, Pallas kernels for 29% -> 20%
where the time goes in v2:
time: 61.9 us; the launch traced here: 61.2 us
  Pallas kernels  42.7 us (69%)
  starting transfers between devices  7.41 us (12%)
  other arithmetic  4.21 us (7%)
  blocking collectives  2.8 us (5%)
  local copies, waits for them, and re-layouts  2.74 us (4%)
  matrix products  1.27 us (2%)
    pallas_call x1, Pallas kernels, summed_signals(): pl.pallas_call(functools.partial(spread_kernel, per, share), out_shape=ja...  30.4 us
    pallas_call x1, Pallas kernels, turned_gains(): pl.pallas_call(functools.partial(gains_kernel, per, blocks), out_shape=ja...  12.3 us
    all_to_all x1, starting transfers between devices, on_device(): got = lax.all_to_all(send, 'gx', split_axis=0, concat_axis=0, tiled=True)  7.41 us
    all_gather x1, blocking collectives, on_device(): got = lax.all_gather(got, 'gy', axis=0, tiled=True)  2.8 us
    transpose x1, local copies, waits for them, and re-layouts, on_device(): summed_signals(per, src, arrival_bins, arrival_fracs, gains)  1.65 us
  transfers between devices with their start and end apart: 1, of which 0 were waited for; matrix products, arithmetic and copies ran while one was open for 0% of the time, Pallas kernels for 20%

profile of v2, /device:TPU:1, one launch (start us, length us, event | category | flops | bytes accessed | tf_op | source)
XLA Modules:
  0.0 61.2 jit_solution(17025362194627653765)
XLA Ops:
  0.0 0.9 %select_reduce_fusion = s32[64]{0:T(128)S(1)} fusion(s32[64]{0:T(128)} %bitcast.20), kind=kLoop, calls=%fused_computation.21 | loop fusion | flops 20416 | bytes 512 | tf_op jit(solution)/shard_map/reduce_sum | solution.py:392
  0.9 0.7 %multiply_add_fusion = s32[64]{0:T(128)S(1)} fusion(s32[64]{0:T(128)S(1)} %select_reduce_fusion, s32[64,1]{0,1:T(1,128)} %param.8), kind=kLoop, calls=%fused_computation.33 | loop fusion | flops 128 | bytes 768 | tf_op jit(solution)/shard_map/add | solution.py:395
  1.6 0.7 %and_select_fusion.1 = (s32[64]{0:T(128)S(1)}, s32[64]{0:T(128)S(1)}) fusion(s32[64]{0:T(128)} %param.9), kind=kLoop, calls=%fused_computation.27 | loop fusion | flops 1216 | bytes 768 | tf_op jit(solution)/shard_map/jit(floor_divide)/jit(_where)/select_n | solution.py:383
  2.3 0.7 %fusion.10 = bf16[64,128]{1,0:T(8,128)(2,1)S(1)} fusion(s32[64]{0:T(128)} %param.10), kind=kLoop, calls=%fused_computation.24 | loop fusion | flops 16384 | bytes 16640 | tf_op jit(solution)/shard_map/convert_element_type | solution.py:376
  3.0 0.9 %broadcast_multiply_fusion = bf16[64,8,128]{2,1,0:T(8,128)(2,1)S(1)} fusion(bf16[64,8,128]{2,1,0:T(8,128)(2,1)} %param.7, bf16[64,128]{1,0:T(8,128)(2,1)S(1)} %fusion.10), kind=kLoop, calls=%fused_computation.16 | loop fusion | flops 65536 | bytes 278528 | tf_op jit(solution)/shard_map/mul | solution.py:379
  3.9 0.1 select_convert_fusion
  4.0 1.0 %fusion = bf16[16,8,1152]{2,1,0:T(8,128)(2,1)} fusion(bf16[64,128]{1,0:T(8,128)(2,1)S(1)} %select_convert_fusion, bf16[64,1024]{1,0:T(8,128)(2,1)S(1)} %bitcast.19, s32[64]{0:T(128)S(1)} %multiply_add_fusion), kind=kOutput, calls=%fused_computation.1 | convolution fusion | flops 19324928 | bytes 442624 | tf_op jit(solution)/shard_map/dot_general | solution.py:397
  5.0 7.4 %all-to-all-start = ((bf16[16,8,1152]{2,1,0:T(8,128)(2,1)}), bf16[16,8,1152]{2,1,0:T(8,128)(2,1)S(1)}, u32[]{:S(2)}, u32[]{:S(2)}) async-start(bf16[16,8,1152]{2,1,0:T(8,128)(2,1)} %fusion), calls=%async_computation | async-start | bytes 589824 | tf_op jit(solution)/shard_map/all_to_all | solution.py:400
  12.4 12.3 %turned_gains.1.gains_hbm = bf16[2,1024,2048]{2,1,0:T(8,128)(2,1)} custom-call(bf16[65536,128]{1,0:T(8,128)(2,1)} %bitcast.15), custom_call_target="tpu_custom_call" | custom-call | flops 4000000000 | bytes 33554432 | tf_op jit(solution)/shard_map/turned_gains/pallas_call | solution.py:99
  24.7 0.0 all-to-all-done
  24.7 2.8 %all_gather.3 = bf16[256,1152]{1,0:T(8,128)(2,1)S(1)} all-gather(bf16[128,1152]{1,0:T(8,128)(2,1)S(1)} %bitcast.16), channel_id=1, replica_groups=mesh['gx'=16,'gy'=2] {'gy'}, dimensions={0}, use_global_device_ids=true | all-gather | bytes 884736 | tf_op jit(solution)/shard_map/all_gather | solution.py:401
  27.6 0.2 fusion.6
  27.8 0.3 convolution_convert_fusion.1
  28.1 1.1 %reshape.84.src_ref = bf16[2048,128]{1,0:T(8,128)(2,1)} reshape(bf16[256,1024]{1,0:T(8,128)(2,1)S(1)} %convolution_convert_fusion.1) | data formatting | bytes 1048576 | tf_op jit(solution)/shard_map/reshape | solution.py:410
  29.2 30.4 %summed_signals.1 = f32[4,32,256]{2,1,0:T(8,128)} custom-call(bf16[2048,128]{1,0:T(8,128)(2,1)} %reshape.84.src_ref, s32[256,4,128]{2,1,0:T(4,128)} %bins_ref.1, f32[256,4,128]{2,1,0:T(4,128)} %fracs_ref.1, bf16[2,1024,2048]{2,1,0:T(8,128)(2,1)} %turned_gains.1.gains_hbm), custom_call_target="tpu_custom_call" | custom-call | tf_op jit(solution)/shard_map/summed_signals/pallas_call | solution.py:338
  59.6 1.6 %copy.16 = f32[32,4,256]{2,1,0:T(4,128)} copy(f32[32,4,256]{2,0,1:T(8,128)} %bitcast.17) | data formatting | bytes 262144 | tf_op jit(solution)/shard_map/transpose | solution.py:413
  (4 shorter events, 0.0 us)
Async XLA Ops:
  5.0 19.7 %all-to-all-start = ((bf16[16,8,1152]{2,1,0:T(8,128)(2,1)}), bf16[16,8,1152]{2,1,0:T(8,128)(2,1)S(1)}, u32[]{:S(2)}, u32[]{:S(2)}) async-start(bf16[16,8,1152]{2,1,0:T(8,128)(2,1)} %fusion), calls=%async_computation | async-start | bytes 589824 | tf_op jit(solution)/shard_map/all_to_all | solution.py:400

commit v3 on v2

v3 whole, which is shorter than its diff:
```python
import functools

import jax
import jax.numpy as jnp
from jax import lax
from jax.experimental import pallas as pl
from jax.experimental.pallas import tpu as pltpu
from jax.sharding import PartitionSpec as P

NBIN = 256
LANES = 128
LO = 64
HI = NBIN // LO
WIDE = LO + 16
CHUNK = 128
SLOTS = 4
UNROLL = 16
MESH = pl.DeviceIdType.MESH


def bf16(v):
    return v.astype(jnp.bfloat16)


def aligned(i, n):
    return pl.multiple_of(i * n, n)


def signals_kernel(
    per, share, cap, sources_ref, owners_ref, owners_row_ref, strip_rows_ref, counts_ref, bins_ref, fracs_ref,
    gains_hbm, out_ref,
    gains, buffer, mixed, work, posted, got_in, row_sums,
    table, arrived, first_out, first_in, kept, last, second_out, second_in, third_out, third_in,
    gain_sems, post_send, post_recv, pass_send, pass_recv,
    one_send, one_recv, two_send, two_recv, three_send, three_recv,
):
    g = lax.axis_index("gx")
    q = lax.axis_index("gy")
    shards = lax.axis_size("gx")
    columns = lax.axis_size("gy")
    depth = shards // 4
    bit0, bit1, z = lax.rem(g, 2), lax.rem(g // 2, 2), g // 4
    flips = (g + 1 - 2 * bit0, g + 2 - 4 * bit1)
    corner = lax.rem(g, 4)
    rows = bins_ref.shape[0]
    wide = columns * share
    tall = depth * wide
    half = NBIN // 2

    observers = gains.shape[1]
    tiles_wide = observers // LANES
    blocks = bins_ref.shape[1]
    deep = tiles_wide * blocks
    group = 256 // deep
    steps = gains.shape[2] // CHUNK
    size = CHUNK * deep

    def fetch(i):
        slot = lax.rem(i, SLOTS)
        return pltpu.make_async_copy(
            gains_hbm.at[pl.ds(aligned(i, size), size)], buffer.at[slot], gain_sems.at[slot]
        )

    for i in range(SLOTS - 1):
        fetch(i).start()

    barrier = pltpu.get_barrier_semaphore()

    def greet(to_g, to_q):
        pl.semaphore_signal(barrier, inc=1, device_id=(to_g, to_q), device_id_type=MESH)

    def others(body):
        def one(i, c):
            to_z, to_q = i // columns, lax.rem(i, columns)

            @pl.when(jnp.logical_or(to_z != z, to_q != q))
            def _():
                body(i, to_z, to_q)

            return c

        lax.fori_loop(0, depth * columns, one, 0)

    def ring(body):
        def one(i, c):
            body(lax.rem(g + i, shards))
            return c

        lax.fori_loop(1, shards, one, 0)

    ring(lambda to_g: greet(to_g, q))

    def beside(body):
        def one(i, c):
            body(lax.rem(q + i, columns))
            return c

        lax.fori_loop(1, columns, one, 0)

    def greet_column(to_q):
        def one(k, c):
            greet(k * 4 + corner, to_q)
            return c

        lax.fori_loop(0, depth, one, 0)

    beside(greet_column)

    strips, terms, panels = sources_ref.shape
    long = terms * panels
    work[...] = sources_ref[...].reshape(strips * terms, panels).astype(jnp.float32)
    before = lax.broadcasted_iota(jnp.int32, (strips, strips), 1) < lax.broadcasted_iota(
        jnp.int32, (strips, strips), 0
    )
    same = jnp.logical_and(owners_ref[...] == owners_row_ref[...], before)
    order = jnp.sum(same.astype(jnp.float32), axis=1, keepdims=True).astype(jnp.int32)
    spot_of = owners_ref[...] * cap + order
    placing = bf16(
        (spot_of == lax.broadcasted_iota(jnp.int32, (strips, shards * cap), 1)).astype(jnp.float32)
    )
    live = lax.broadcasted_iota(jnp.int32, (strips, panels), 1) < counts_ref[...]
    pieces = [
        bf16(jnp.where(live, work[pl.ds(k, strips, stride=terms), :], 0.0)) for k in range(terms)
    ]
    labels = (strip_rows_ref[...] + 1).astype(jnp.float32)
    pieces.append(
        bf16(jnp.where(lax.broadcasted_iota(jnp.int32, (strips, LANES), 1) == 0, labels, 0.0))
    )
    placed = bf16(
        lax.dot_general(
            placing,
            jnp.concatenate(pieces, axis=1),
            (((0,), (0,)), ((), ())),
            preferred_element_type=jnp.float32,
        )
    )
    posted[...] = placed.reshape(shards, cap, long + LANES)

    def post(to_g):
        return pltpu.make_async_remote_copy(
            src_ref=posted.at[to_g],
            dst_ref=got_in.at[q, g],
            send_sem=post_send.at[to_g],
            recv_sem=post_recv.at[g],
            device_id=(to_g, q),
            device_id_type=MESH,
        )

    def posted_by(from_g):
        return pltpu.make_async_remote_copy(
            src_ref=posted.at[from_g],
            dst_ref=got_in.at[q, from_g],
            send_sem=post_send.at[from_g],
            recv_sem=post_recv.at[from_g],
            device_id=(from_g, q),
            device_id_type=MESH,
        )

    def hand(from_g, to_q):
        return pltpu.make_async_remote_copy(
            src_ref=got_in.at[q, from_g],
            dst_ref=got_in.at[q, from_g],
            send_sem=pass_send.at[to_q, from_g],
            recv_sem=pass_recv.at[q, from_g],
            device_id=(g, to_q),
            device_id_type=MESH,
        )

    def handed_by(from_g, from_q):
        return pltpu.make_async_remote_copy(
            src_ref=got_in.at[from_q, from_g],
            dst_ref=got_in.at[from_q, from_g],
            send_sem=pass_send.at[from_q, from_g],
            recv_sem=pass_recv.at[from_q, from_g],
            device_id=(g, from_q),
            device_id_type=MESH,
        )

    pl.semaphore_wait(barrier, shards - 1 + depth * (columns - 1))
    ring(lambda to_g: post(to_g).start())
    got_in[q, g] = posted[g]
    beside(lambda to_q: hand(g, to_q).start())

    height = per * tiles_wide * group
    row = lax.broadcasted_iota(jnp.int32, (height, 256), 0)
    spot = lax.broadcasted_iota(jnp.int32, (height, 256), 1)
    wanted = (
        lax.rem(row, group) * deep
        + lax.rem(row // group, tiles_wide) * blocks
        + q * per
        + row // (group * tiles_wide)
    )
    pick = bf16((wanted == spot).astype(jnp.float32))

    def turn(i, carry):
        slot = lax.rem(i, SLOTS)

        @pl.when(i + SLOTS - 1 < steps)
        def _():
            fetch(i + SLOTS - 1).start()

        fetch(i).wait()

        def part(j, c):
            one = buffer[slot, pl.ds(aligned(j, 512), 256), :]
            two = buffer[slot, pl.ds(aligned(j, 512) + 256, 256), :]
            got = jnp.dot(
                pick, jnp.concatenate([one, two], axis=1), preferred_element_type=jnp.float32
            )
            for o in range(per):
                for t in range(tiles_wide):
                    at = (o * tiles_wide + t) * group
                    both = jnp.concatenate(
                        [got[at : at + group, :LANES], got[at : at + group, LANES:]], axis=0
                    )
                    mixed[
                        o, pl.ds(aligned(j, 2 * group), 2 * group), t * LANES : (t + 1) * LANES
                    ] = bf16(both)
            return c

        lax.fori_loop(0, CHUNK // (2 * group), part, 0, unroll=True)
        for o in range(per):
            for t in range(tiles_wide):
                gains[o, t * LANES : (t + 1) * LANES, pl.ds(aligned(i, CHUNK), CHUNK)] = mixed[
                    o, :, t * LANES : (t + 1) * LANES
                ].T
        return carry

    lax.fori_loop(0, steps, turn, 0)

    spots = bf16(lax.broadcasted_iota(jnp.int32, (WIDE, LANES), 0).astype(jnp.float32))
    lane = lax.broadcasted_iota(jnp.int32, (16, LANES), 1)
    upper = lax.broadcasted_iota(jnp.int32, (16, LANES), 0) < 8
    zero = jnp.zeros((), jnp.bfloat16)

    def prepare(j):
        block = q * per + j
        bins = bins_ref[:, pl.ds(block, 1), :].reshape(rows, LANES)
        fracs = fracs_ref[:, pl.ds(block, 1), :].reshape(rows, LANES)
        table[j, 0] = (bins // LO).astype(jnp.float32)
        table[j, 1] = lax.rem(bins, LO).astype(jnp.float32)
        table[j, 2] = 1.0 - fracs
        table[j, 3] = fracs

    def scatter(j):
        def spread(kind, row, n):
            return jnp.broadcast_to(table[j, kind, pl.ds(row, 1), :], (n, LANES))

        def weights_of(row):
            low = spread(1, row, WIDE)
            return jnp.where(
                spots == bf16(low),
                bf16(spread(2, row, WIDE)),
                jnp.where(spots == bf16(low + 1.0), bf16(spread(3, row, WIDE)), zero),
            )

        def pair(i, carry):
            both = bf16(row_sums[pl.ds(aligned(i, 16), 16), :])
            left = bf16(jnp.where(upper, spread(0, 2 * i, 16), -1.0))
            right = bf16(jnp.where(upper, -1.0, spread(0, 2 * i + 1, 16)))
            lhs = []
            for h in range(HI):
                at = jnp.asarray(h, jnp.bfloat16)
                lhs.append(
                    jnp.concatenate(
                        [jnp.where(left == at, both, zero), jnp.where(right == at, both, zero)], axis=1
                    )
                )
            rhs = jnp.concatenate([weights_of(2 * i), weights_of(2 * i + 1)], axis=1)
            got = lax.dot_general(
                jnp.concatenate(lhs, axis=0), rhs, (((1,), (1,)), ((), ())), preferred_element_type=jnp.float32
            )
            got = jnp.concatenate([got, jnp.zeros((16 * HI, LANES - WIDE), jnp.float32)], axis=1)
            tiles = []
            carried = None
            for t in range(NBIN // LANES):
                even = got[32 * t : 32 * t + 16, :]
                odd = pltpu.roll(got[32 * t + 16 : 32 * t + 32, :], LO, 1)
                tile = even + jnp.where(lane >= LO, odd, 0.0)
                if carried is not None:
                    tile = tile + jnp.where(lane < LO, carried, 0.0)
                carried = odd
                tiles.append(tile)
            arrived[pl.ds(aligned(i, 16), 16), :] = bf16(jnp.concatenate(tiles, axis=1))
            return carry

        lax.fori_loop(0, rows // 2, pair, 0, unroll=UNROLL)

    def multiply(j, c0, c1):
        lhs = jnp.concatenate(
            [
                gains[j, pl.ds(pl.multiple_of((k * 4 + c1 * 2 + c0) * wide, 8), wide), :]
                for k in range(depth)
            ],
            axis=0,
        )
        return jnp.dot(lhs, arrived[...], preferred_element_type=jnp.float32)

    def stage_one(j, h, part):
        return pltpu.make_async_remote_copy(
            src_ref=first_out.at[j, h, part],
            dst_ref=first_in.at[j, h, part],
            send_sem=one_send.at[j, h, part],
            recv_sem=one_recv.at[j, h, part],
            device_id=(flips[h], q),
            device_id_type=MESH,
        )

    def stage_two(j, h):
        return pltpu.make_async_remote_copy(
            src_ref=second_out.at[j, h],
            dst_ref=second_in.at[j, h],
            send_sem=two_send.at[j, h],
            recv_sem=two_recv.at[j, h],
            device_id=(flips[1 - h], q),
            device_id_type=MESH,
        )

    def stage_three(j, i, to_z, to_q):
        return pltpu.make_async_remote_copy(
            src_ref=third_out.at[j, i],
            dst_ref=third_in.at[j, z * columns + q],
            send_sem=three_send.at[j, i],
            recv_sem=three_recv.at[j, z * columns + q],
            device_id=(to_z * 4 + corner, to_q),
            device_id_type=MESH,
        )

    def arrival(j, i):
        return pltpu.make_async_remote_copy(
            src_ref=third_out.at[j, i],
            dst_ref=third_in.at[j, i],
            send_sem=three_send.at[j, i],
            recv_sem=three_recv.at[j, i],
            device_id=((i // columns) * 4 + corner, lax.rem(i, columns)),
            device_id_type=MESH,
        )

    sides = (slice(0, half), slice(half, NBIN))

    def products(j):
        got = multiply(j, 1 - bit0, 1 - bit1)
        for h in range(2):
            first_out[j, h, 0] = bf16(got[:, sides[h]])
            stage_one(j, h, 0).start()
        got = multiply(j, 1 - bit0, bit1)
        first_out[j, 0, 1] = bf16(got[:, sides[0]])
        stage_one(j, 0, 1).start()
        kept[j, 1] = got[:, sides[1]]
        got = multiply(j, bit0, 1 - bit1)
        first_out[j, 1, 1] = bf16(got[:, sides[1]])
        stage_one(j, 1, 1).start()
        kept[j, 0] = got[:, sides[0]]
        got = multiply(j, bit0, bit1)
        for h in range(2):
            last[j, h] = got[:, sides[h]]

    for j in range(per):
        prepare(j)

    def relay(from_g):
        posted_by(from_g).wait_recv()
        beside(lambda to_q: hand(from_g, to_q).start())

    ring(relay)

    def every(body):
        def one(i, c):
            body(i)
            return c

        lax.fori_loop(0, shards, one, 0)

    beside(lambda from_q: every(lambda from_g: handed_by(from_g, from_q).wait_recv()))
    slots = columns * shards * cap
    letters = got_in[...].reshape(slots, long + LANES)
    labels = letters[:, long:].astype(jnp.float32)[:, :1] - 1.0
    hot = bf16(
        (labels == lax.broadcasted_iota(jnp.int32, (slots, rows), 1).astype(jnp.float32)).astype(jnp.float32)
    )
    summed = lax.dot_general(
        hot, letters[:, :long], (((0,), (0,)), ((), ())), preferred_element_type=jnp.float32
    )
    for k in range(terms):
        row_sums[pl.ds(k, rows, stride=terms), :] = summed[:, k * panels : (k + 1) * panels]
    for j in range(per):
        scatter(j)
        products(j)
    for j in range(per):
        for h in range(2):
            stage_one(j, h, 0).wait_recv()
            second_out[j, h] = bf16(kept[j, h] + first_in[j, h, 0].astype(jnp.float32))
            stage_two(j, h).start()
    for j in range(per):
        for h in range(2):
            stage_one(j, h, 1).wait_recv()
            stage_two(j, h).wait_recv()
            total = (
                last[j, h]
                + first_in[j, h, 1].astype(jnp.float32)
                + second_in[j, h].astype(jnp.float32)
            )
            third_out[j, :, :, sides[h]] = bf16(total).reshape(depth * columns, share, half)
        others(lambda i, to_z, to_q: stage_three(j, i, to_z, to_q).start())
        third_in[j, z * columns + q] = third_out[j, z * columns + q]
    for j in range(per):
        others(lambda i, to_z, to_q: arrival(j, i).wait_recv())
        for c in range(columns):
            total = third_in[j, c].astype(jnp.float32)
            for k in range(1, depth):
                total = total + third_in[j, k * columns + c].astype(jnp.float32)
            out_ref[c * per + j] = total
    for j in range(per):
        for h in range(2):
            for part in range(2):
                stage_one(j, h, part).wait_send()
            stage_two(j, h).wait_send()
        others(lambda i, to_z, to_q: stage_three(j, i, to_z, to_q).wait_send())
    ring(lambda to_g: post(to_g).wait_send())
    beside(lambda to_q: every(lambda from_g: hand(from_g, to_q).wait_send()))


def on_device(sources, owners, strip_rows, panel_counts, arrival_bins, arrival_fracs, gain_table):
    strips, terms, panels = sources.shape
    shards, columns = lax.axis_size("gx"), lax.axis_size("gy")
    cap = 2 * strips // shards
    rows, blocks = arrival_bins.shape[:2]
    observers = gain_table.shape[3]
    per = blocks // columns
    share = observers // (shards * columns)
    peers = shards // 4 * columns
    tall = peers * share
    half = NBIN // 2
    tiles_wide = observers // LANES
    wide = terms * panels + LANES
    assert panels == LANES and rows <= 256 and terms == 8
    flat = (
        gain_table.reshape(rows * terms, blocks, tiles_wide, LANES).transpose(0, 2, 1, 3).reshape(-1, LANES)
    )
    dma = pltpu.SemaphoreType.DMA
    signals = pl.pallas_call(
        functools.partial(signals_kernel, per, share, cap),
        out_shape=jax.ShapeDtypeStruct((blocks, share, NBIN), jnp.float32),
        in_specs=[pl.BlockSpec(memory_space=pltpu.VMEM)] * 7 + [pl.BlockSpec(memory_space=pl.ANY)],
        out_specs=pl.BlockSpec(memory_space=pltpu.VMEM),
        scratch_shapes=[
            pltpu.VMEM((per, observers, rows * terms), jnp.bfloat16),
            pltpu.VMEM((SLOTS, CHUNK * tiles_wide * blocks, LANES), jnp.bfloat16),
            pltpu.VMEM((per, CHUNK, observers), jnp.bfloat16),
            pltpu.VMEM((strips * terms, panels), jnp.float32),
            pltpu.VMEM((shards, cap, wide), jnp.bfloat16),
            pltpu.VMEM((columns, shards, cap, wide), jnp.bfloat16),
            pltpu.VMEM((rows * terms, panels), jnp.float32),
            pltpu.VMEM((per, 4, rows, LANES), jnp.float32),
            pltpu.VMEM((rows * terms, NBIN), jnp.bfloat16),
            pltpu.VMEM((per, 2, 2, tall, half), jnp.bfloat16),
            pltpu.VMEM((per, 2, 2, tall, half), jnp.bfloat16),
            pltpu.VMEM((per, 2, tall, half), jnp.float32),
            pltpu.VMEM((per, 2, tall, half), jnp.float32),
            pltpu.VMEM((per, 2, tall, half), jnp.bfloat16),
            pltpu.VMEM((per, 2, tall, half), jnp.bfloat16),
            pltpu.VMEM((per, peers, share, NBIN), jnp.bfloat16),
            pltpu.VMEM((per, peers, share, NBIN), jnp.bfloat16),
            dma((SLOTS,)),
            dma((shards,)),
            dma((shards,)),
            dma((columns, shards)),
            dma((columns, shards)),
            dma((per, 2, 2)),
            dma((per, 2, 2)),
            dma((per, 2)),
            dma((per, 2)),
            dma((per, peers)),
            dma((per, peers)),
        ],
        compiler_params=pltpu.CompilerParams(collective_id=0, has_side_effects=True),
        name="signals",
    )(
        sources,
        owners,
        owners.reshape(1, strips),
        strip_rows.reshape(strips, 1),
        panel_counts.reshape(strips, 1),
        arrival_bins,
        arrival_fracs,
        flat,
    )
    return signals.transpose(1, 0, 2)


def solution(mesh):
    placed = (
        P(("gx", "gy"), None, None),
        P(("gx", "gy"), None),
        P(("gx", "gy")),
        P(("gx", "gy")),
        P("gx", None, None),
        P("gx", None, None),
        P("gx", None, None, None),
    )
    return jax.shard_map(
        on_device,
        mesh=mesh,
        in_specs=placed,
        out_specs=P(("gx", "gy"), None, None),
        check_vma=False,
    )
```

time: 61.9 us -> 50.1 us (0.81)
  starting transfers between devices: 7.41 us -> 0 us
  other arithmetic: 4.21 us -> 0 us
  local copies, waits for them, and re-layouts: 2.74 us -> 5.7 us
  blocking collectives: 2.8 us -> 0 us
  matrix products: 1.27 us -> 0 us
  Pallas kernels: 42.7 us -> 43.9 us
    all_to_all x1 -> x0, starting transfers between devices: 7.41 us -> none  [on_device(): got = lax.all_to_all(send, 'gx', split_axis=0, concat_axis=0, tiled=True)]
    all_gather x1 -> x0, blocking collectives: 2.8 us -> none  [on_device(): got = lax.all_gather(got, 'gy', axis=0, tiled=True)]
    reshape x1 -> x2, local copies, waits for them, and re-layouts: 1.07 us -> 2.69 us  [the longest x1 1.35 us: on_device(): panel_counts.reshape(strips, 1)]
    unnamed x1, local copies, waits for them, and re-layouts: 0.02 us -> 1.36 us
    dot_general x2 -> x0, matrix products: 1.27 us -> none  [the longest x1 0.96 us: on_device(): jnp.dot(placing.astype(jnp.bfloat16), payload, preferred_element_type=jnp...]
    pallas_call x2 -> x1, Pallas kernels: 42.7 us -> 43.9 us  [on_device(): pl.pallas_call(functools.partial(signals_kernel, per, share, cap), out_sh...]
    mul x1 -> x0, other arithmetic: 0.93 us -> none  [on_device(): sources * live_mask[:, None, :]]
    reduce_sum x1 -> x0, other arithmetic: 0.91 us -> none  [on_device(): jnp.sum(jnp.where(earlier & (targets[None, :] == targets[:, None]), 1, 0)...]
  transfers between devices with their start and end apart: 1 -> 0, of which waited for: 0 -> 0; matrix products, arithmetic and copies ran while one was open for 0% -> 0% of each run, Pallas kernels for 20% -> 0%
where the time goes in v3:
time: 50.1 us; the launch traced here: 49.6 us
  Pallas kernels  43.9 us (88%)
  local copies, waits for them, and re-layouts  5.7 us (11%)
    pallas_call x1, Pallas kernels, on_device(): pl.pallas_call(functools.partial(signals_kernel, per, share, cap), out_sh...  43.9 us
    transpose x1, local copies, waits for them, and re-layouts, on_device(): return signals.transpose(1, 0, 2)  1.65 us
    unnamed x1, local copies, waits for them, and re-layouts  1.36 us
    reshape x1, local copies, waits for them, and re-layouts, on_device(): panel_counts.reshape(strips, 1)  1.35 us
    reshape x1, local copies, waits for them, and re-layouts, on_device(): strip_rows.reshape(strips, 1)  1.34 us

profile of v3, /device:TPU:1, one launch (start us, length us, event | category | flops | bytes accessed | tf_op | source)
XLA Modules:
  0.0 49.6 jit_solution(10436046671795590157)
XLA Ops:
  0.0 1.3 %copy.10.strip_rows_ref = s32[64,1]{1,0:T(8,128)} copy(s32[64,1]{0,1:T(1,128)} %bitcast.12) | data formatting | bytes 512 | tf_op jit(solution)/shard_map/reshape | solution.py:482
  1.3 1.4 %copy.11.counts_ref = s32[64,1]{1,0:T(8,128)} copy(s32[64,1]{0,1:T(1,128)} %bitcast.13) | data formatting | bytes 512 | tf_op jit(solution)/shard_map/reshape | solution.py:483
  2.7 1.4 %copy.9.owners_ref = s32[64,1]{1,0:T(8,128)} copy(s32[64,1]{0,1:T(1,128)} %param.8) | data formatting | bytes 512 | tf_op args[1]
  4.1 43.9 %signals.1 = f32[4,32,256]{2,1,0:T(8,128)} custom-call(bf16[64,8,128]{2,1,0:T(8,128)(2,1)} %sources_ref.1, s32[64,1]{1,0:T(8,128)} %copy.9.owners_ref, s32[1,64]{1,0:T(1,128)} %bitcast.11, s32[64,1]{1,0:T(8,128)} %copy.10.strip_rows_ref, s32[64,1]{1,0:T(8,128)} %copy.11.counts_ref, s32[256,4,128]{2,1,0:T(4,128)} %bins_ref.1, f32[256,4,128]{2,1,0:T(4,128)} %fracs_ref.1, ...), custom_call_target="tpu_custom_call" | custom-call | tf_op jit(solution)/shard_map/signals/pallas_call | solution.py:441
  48.0 1.6 %copy.12 = f32[32,4,256]{2,1,0:T(4,128)} copy(f32[32,4,256]{2,0,1:T(8,128)} %bitcast.10) | data formatting | bytes 262144 | tf_op jit(solution)/shard_map/transpose | solution.py:488

commit v4 on v3

--- a/solution.py
+++ b/solution.py
@@ -27,7 +27,7 @@
 
 
 def signals_kernel(
-    per, share, cap, sources_ref, owners_ref, owners_row_ref, strip_rows_ref, counts_ref, bins_ref, fracs_ref,
+    per, share, cap, sources_ref, owners_ref, strip_rows_ref, counts_ref, bins_ref, fracs_ref,
     gains_hbm, out_ref,
     gains, buffer, mixed, work, posted, got_in, row_sums,
     table, arrived, first_out, first_in, kept, last, second_out, second_in, third_out, third_in,
@@ -112,17 +112,26 @@
     before = lax.broadcasted_iota(jnp.int32, (strips, strips), 1) < lax.broadcasted_iota(
         jnp.int32, (strips, strips), 0
     )
-    same = jnp.logical_and(owners_ref[...] == owners_row_ref[...], before)
-    order = jnp.sum(same.astype(jnp.float32), axis=1, keepdims=True).astype(jnp.int32)
-    spot_of = owners_ref[...] * cap + order
+    eye = lax.broadcasted_iota(jnp.int32, (strips, strips), 1) == lax.broadcasted_iota(
+        jnp.int32, (strips, strips), 0
+    )
+
+    def stood(ref):
+        row = ref[...].astype(jnp.float32)
+        return jnp.sum(jnp.where(eye, jnp.broadcast_to(row, eye.shape), 0.0), axis=1, keepdims=True)
+
+    targets = stood(owners_ref)
+    same = jnp.logical_and(targets == owners_ref[...].astype(jnp.float32), before)
+    order = jnp.sum(same.astype(jnp.float32), axis=1, keepdims=True)
+    spot_of = (targets * cap + order).astype(jnp.int32)
     placing = bf16(
         (spot_of == lax.broadcasted_iota(jnp.int32, (strips, shards * cap), 1)).astype(jnp.float32)
     )
-    live = lax.broadcasted_iota(jnp.int32, (strips, panels), 1) < counts_ref[...]
+    live = lax.broadcasted_iota(jnp.int32, (strips, panels), 1).astype(jnp.float32) < stood(counts_ref)
     pieces = [
         bf16(jnp.where(live, work[pl.ds(k, strips, stride=terms), :], 0.0)) for k in range(terms)
     ]
-    labels = (strip_rows_ref[...] + 1).astype(jnp.float32)
+    labels = stood(strip_rows_ref) + 1.0
     pieces.append(
         bf16(jnp.where(lax.broadcasted_iota(jnp.int32, (strips, LANES), 1) == 0, labels, 0.0))
     )
@@ -242,7 +251,7 @@
         table[j, 2] = 1.0 - fracs
         table[j, 3] = fracs
 
-    def scatter(j):
+    def scatter(j, low, high):
         def spread(kind, row, n):
             return jnp.broadcast_to(table[j, kind, pl.ds(row, 1), :], (n, LANES))
 
@@ -284,7 +293,7 @@
             arrived[pl.ds(aligned(i, 16), 16), :] = bf16(jnp.concatenate(tiles, axis=1))
             return carry
 
-        lax.fori_loop(0, rows // 2, pair, 0, unroll=UNROLL)
+        lax.fori_loop(low, high, pair, 0, unroll=UNROLL)
 
     def multiply(j, c0, c1):
         lhs = jnp.concatenate(
@@ -383,15 +392,13 @@
     )
     for k in range(terms):
         row_sums[pl.ds(k, rows, stride=terms), :] = summed[:, k * panels : (k + 1) * panels]
-    for j in range(per):
-        scatter(j)
-        products(j)
-    for j in range(per):
+    def second(j):
         for h in range(2):
             stage_one(j, h, 0).wait_recv()
             second_out[j, h] = bf16(kept[j, h] + first_in[j, h, 0].astype(jnp.float32))
             stage_two(j, h).start()
-    for j in range(per):
+
+    def third(j):
         for h in range(2):
             stage_one(j, h, 1).wait_recv()
             stage_two(j, h).wait_recv()
@@ -403,13 +410,27 @@
             third_out[j, :, :, sides[h]] = bf16(total).reshape(depth * columns, share, half)
         others(lambda i, to_z, to_q: stage_three(j, i, to_z, to_q).start())
         third_in[j, z * columns + q] = third_out[j, z * columns + q]
+
+    pairs = rows // 2
+    for j in range(per):
+        if j == 0:
+            scatter(j, 0, pairs)
+        else:
+            scatter(j, 0, pairs // 2)
+            second(j - 1)
+            scatter(j, pairs // 2, pairs)
+        products(j)
+        if j > 0:
+            third(j - 1)
+    second(per - 1)
+    third(per - 1)
     for j in range(per):
         others(lambda i, to_z, to_q: arrival(j, i).wait_recv())
         for c in range(columns):
             total = third_in[j, c].astype(jnp.float32)
             for k in range(1, depth):
                 total = total + third_in[j, k * columns + c].astype(jnp.float32)
-            out_ref[c * per + j] = total
+            out_ref[:, c * per + j, :] = total
     for j in range(per):
         for h in range(2):
             for part in range(2):
@@ -438,10 +459,10 @@
         gain_table.reshape(rows * terms, blocks, tiles_wide, LANES).transpose(0, 2, 1, 3).reshape(-1, LANES)
     )
     dma = pltpu.SemaphoreType.DMA
-    signals = pl.pallas_call(
+    return pl.pallas_call(
         functools.partial(signals_kernel, per, share, cap),
-        out_shape=jax.ShapeDtypeStruct((blocks, share, NBIN), jnp.float32),
-        in_specs=[pl.BlockSpec(memory_space=pltpu.VMEM)] * 7 + [pl.BlockSpec(memory_space=pl.ANY)],
+        out_shape=jax.ShapeDtypeStruct((share, blocks, NBIN), jnp.float32),
+        in_specs=[pl.BlockSpec(memory_space=pltpu.VMEM)] * 6 + [pl.BlockSpec(memory_space=pl.ANY)],
         out_specs=pl.BlockSpec(memory_space=pltpu.VMEM),
         scratch_shapes=[
             pltpu.VMEM((per, observers, rows * terms), jnp.bfloat16),
@@ -477,15 +498,13 @@
         name="signals",
     )(
         sources,
-        owners,
         owners.reshape(1, strips),
-        strip_rows.reshape(strips, 1),
-        panel_counts.reshape(strips, 1),
+        strip_rows.reshape(1, strips),
+        panel_counts.reshape(1, strips),
         arrival_bins,
         arrival_fracs,
         flat,
     )
-    return signals.transpose(1, 0, 2)
 
 
 def solution(mesh):

time: 50.1 us -> 44.7 us (0.89)
  local copies, waits for them, and re-layouts: 5.7 us -> 1.57 us
  Pallas kernels: 43.9 us -> 42.6 us
    reshape x2 -> x0, local copies, waits for them, and re-layouts: 2.69 us -> none  [the longest x1 1.35 us: on_device(): panel_counts.reshape(strips, 1)]
    transpose x1 -> x0, local copies, waits for them, and re-layouts: 1.65 us -> none  [on_device(): return signals.transpose(1, 0, 2)]
    pallas_call x1, Pallas kernels: 43.9 us -> 42.6 us  [on_device(): pl.pallas_call(functools.partial(signals_kernel, per, share, cap), out_sh...]
where the time goes in v4:
time: 44.7 us; the launch traced here: 44.2 us
  Pallas kernels  42.6 us (95%)
  local copies, waits for them, and re-layouts  1.57 us (4%)
    pallas_call x1, Pallas kernels, on_device(): pl.pallas_call(functools.partial(signals_kernel, per, share, cap), out_sh...  42.6 us
    unnamed x1, local copies, waits for them, and re-layouts  1.57 us

profile of v4, /device:TPU:1, one launch (start us, length us, event | category | flops | bytes accessed | tf_op | source)
XLA Modules:
  0.0 44.2 jit_solution(2976101621097937836)
XLA Ops:
  0.0 42.6 %signals.1 = f32[32,4,256]{2,1,0:T(4,128)} custom-call(bf16[64,8,128]{2,1,0:T(8,128)(2,1)} %sources_ref.1, s32[1,64]{1,0:T(1,128)} %bitcast.9, s32[1,64]{1,0:T(1,128)} %bitcast.10, s32[1,64]{1,0:T(1,128)} %bitcast.11, s32[256,4,128]{2,1,0:T(4,128)} %bins_ref.1, f32[256,4,128]{2,1,0:T(4,128)} %fracs_ref.1, bf16[65536,128]{1,0:T(8,128)(2,1)} %bitcast.8), custom_call_target="tpu_custom_call" | custom-call | tf_op jit(solution)/shard_map/signals/pallas_call | solution.py:462
  42.6 1.6 %copy.10 = f32[32,4,256]{2,1,0:T(4,128)} copy(f32[32,4,256]{2,1,0:T(4,128)} %signals.1) | data formatting | bytes 262144

commit v5 on v4

--- a/solution.py
+++ b/solution.py
@@ -10,11 +10,12 @@
 NBIN = 256
 LANES = 128
 LO = 64
+LO_BITS = LO.bit_length() - 1
 HI = NBIN // LO
 WIDE = LO + 16
 CHUNK = 128
 SLOTS = 4
-UNROLL = 16
+UNROLL = 64
 MESH = pl.DeviceIdType.MESH
 
 
@@ -27,11 +28,11 @@
 
 
 def signals_kernel(
-    per, share, cap, sources_ref, owners_ref, strip_rows_ref, counts_ref, bins_ref, fracs_ref,
-    gains_hbm, out_ref,
+    per, share, cap, sources_ref, owners_ref, strip_rows_ref, counts_ref,
+    bins_hbm, fracs_hbm, gains_hbm, out_ref,
     gains, buffer, mixed, work, posted, got_in, row_sums,
-    table, arrived, first_out, first_in, kept, last, second_out, second_in, third_out, third_in,
-    gain_sems, post_send, post_recv, pass_send, pass_recv,
+    bins, fracs, arrived, first_out, first_in, kept, last, second_out, second_in, third_out, third_in,
+    gain_sems, table_sems, post_send, post_recv, pass_send, pass_recv,
     one_send, one_recv, two_send, two_recv, three_send, three_recv,
 ):
     g = lax.axis_index("gx")
@@ -42,14 +43,14 @@
     bit0, bit1, z = lax.rem(g, 2), lax.rem(g // 2, 2), g // 4
     flips = (g + 1 - 2 * bit0, g + 2 - 4 * bit1)
     corner = lax.rem(g, 4)
-    rows = bins_ref.shape[0]
+    rows = row_sums.shape[0] // 8
     wide = columns * share
     tall = depth * wide
     half = NBIN // 2
 
     observers = gains.shape[1]
     tiles_wide = observers // LANES
-    blocks = bins_ref.shape[1]
+    blocks = per * columns
     deep = tiles_wide * blocks
     group = 256 // deep
     steps = gains.shape[2] // CHUNK
@@ -63,6 +64,12 @@
 
     for i in range(SLOTS - 1):
         fetch(i).start()
+    tables = (
+        pltpu.make_async_copy(bins_hbm, bins, table_sems.at[0]),
+        pltpu.make_async_copy(fracs_hbm, fracs, table_sems.at[1]),
+    )
+    for table in tables:
+        table.start()
 
     barrier = pltpu.get_barrier_semaphore()
 
@@ -186,7 +193,13 @@
         )
 
     pl.semaphore_wait(barrier, shards - 1 + depth * (columns - 1))
-    ring(lambda to_g: post(to_g).start())
+    turn_round = jnp.where(z * 2 < depth, shards - 1, 1)
+
+    def far_first(i, c):
+        post(lax.rem(g + i * turn_round, shards)).start()
+        return c
+
+    lax.fori_loop(1, shards, far_first, 0)
     got_in[q, g] = posted[g]
     beside(lambda to_q: hand(g, to_q).start())
 
@@ -236,37 +249,36 @@
         return carry
 
     lax.fori_loop(0, steps, turn, 0)
+    for table in tables:
+        table.wait()
 
     spots = bf16(lax.broadcasted_iota(jnp.int32, (WIDE, LANES), 0).astype(jnp.float32))
     lane = lax.broadcasted_iota(jnp.int32, (16, LANES), 1)
     upper = lax.broadcasted_iota(jnp.int32, (16, LANES), 0) < 8
     zero = jnp.zeros((), jnp.bfloat16)
 
-    def prepare(j):
+    def scatter(j, low, high):
         block = q * per + j
-        bins = bins_ref[:, pl.ds(block, 1), :].reshape(rows, LANES)
-        fracs = fracs_ref[:, pl.ds(block, 1), :].reshape(rows, LANES)
-        table[j, 0] = (bins // LO).astype(jnp.float32)
-        table[j, 1] = lax.rem(bins, LO).astype(jnp.float32)
-        table[j, 2] = 1.0 - fracs
-        table[j, 3] = fracs
-
-    def scatter(j, low, high):
-        def spread(kind, row, n):
-            return jnp.broadcast_to(table[j, kind, pl.ds(row, 1), :], (n, LANES))
+
+        def spread(ref, row, n):
+            return jnp.broadcast_to(ref[pl.ds(row * blocks + block, 1), :], (n, LANES))
 
         def weights_of(row):
-            low = spread(1, row, WIDE)
+            frac = spread(fracs, row, WIDE)
+            low = (spread(bins, row, WIDE) & (LO - 1)).astype(jnp.float32)
             return jnp.where(
                 spots == bf16(low),
-                bf16(spread(2, row, WIDE)),
-                jnp.where(spots == bf16(low + 1.0), bf16(spread(3, row, WIDE)), zero),
+                bf16(1.0 - frac),
+                jnp.where(spots == bf16(low + 1.0), bf16(frac), zero),
             )
+
+        def high_of(row):
+            return (spread(bins, row, 16) >> LO_BITS).astype(jnp.float32)
 
         def pair(i, carry):
             both = bf16(row_sums[pl.ds(aligned(i, 16), 16), :])
-            left = bf16(jnp.where(upper, spread(0, 2 * i, 16), -1.0))
-            right = bf16(jnp.where(upper, -1.0, spread(0, 2 * i + 1, 16)))
+            left = bf16(jnp.where(upper, high_of(2 * i), -1.0))
+            right = bf16(jnp.where(upper, -1.0, high_of(2 * i + 1)))
             lhs = []
             for h in range(HI):
                 at = jnp.asarray(h, jnp.bfloat16)
@@ -363,9 +375,6 @@
         got = multiply(j, bit0, bit1)
         for h in range(2):
             last[j, h] = got[:, sides[h]]
-
-    for j in range(per):
-        prepare(j)
 
     def relay(from_g):
         posted_by(from_g).wait_recv()
@@ -462,7 +471,7 @@
     return pl.pallas_call(
         functools.partial(signals_kernel, per, share, cap),
         out_shape=jax.ShapeDtypeStruct((share, blocks, NBIN), jnp.float32),
-        in_specs=[pl.BlockSpec(memory_space=pltpu.VMEM)] * 6 + [pl.BlockSpec(memory_space=pl.ANY)],
+        in_specs=[pl.BlockSpec(memory_space=pltpu.VMEM)] * 4 + [pl.BlockSpec(memory_space=pl.ANY)] * 3,
         out_specs=pl.BlockSpec(memory_space=pltpu.VMEM),
         scratch_shapes=[
             pltpu.VMEM((per, observers, rows * terms), jnp.bfloat16),
@@ -472,7 +481,8 @@
             pltpu.VMEM((shards, cap, wide), jnp.bfloat16),
             pltpu.VMEM((columns, shards, cap, wide), jnp.bfloat16),
             pltpu.VMEM((rows * terms, panels), jnp.float32),
-            pltpu.VMEM((per, 4, rows, LANES), jnp.float32),
+            pltpu.VMEM((rows * blocks, LANES), jnp.int32),
+            pltpu.VMEM((rows * blocks, LANES), jnp.float32),
             pltpu.VMEM((rows * terms, NBIN), jnp.bfloat16),
             pltpu.VMEM((per, 2, 2, tall, half), jnp.bfloat16),
             pltpu.VMEM((per, 2, 2, tall, half), jnp.bfloat16),
@@ -483,6 +493,7 @@
             pltpu.VMEM((per, peers, share, NBIN), jnp.bfloat16),
             pltpu.VMEM((per, peers, share, NBIN), jnp.bfloat16),
             dma((SLOTS,)),
+            dma((2,)),
             dma((shards,)),
             dma((shards,)),
             dma((columns, shards)),
@@ -501,8 +512,8 @@
         owners.reshape(1, strips),
         strip_rows.reshape(1, strips),
         panel_counts.reshape(1, strips),
-        arrival_bins,
-        arrival_fracs,
+        arrival_bins.reshape(-1, panels),
+        arrival_fracs.reshape(-1, panels),
         flat,
     )
 

time: 44.7 us -> 39.8 us (0.89)
  Pallas kernels: 42.6 us -> 38 us
    pallas_call x1, Pallas kernels: 42.6 us -> 38 us  [on_device(): pl.pallas_call(functools.partial(signals_kernel, per, share, cap), out_sh...]
where the time goes in v5:
time: 39.8 us; the launch traced here: 39.6 us
  Pallas kernels  38 us (95%)
  local copies, waits for them, and re-layouts  1.57 us (4%)
    pallas_call x1, Pallas kernels, on_device(): pl.pallas_call(functools.partial(signals_kernel, per, share, cap), out_sh...  38 us
    unnamed x1, local copies, waits for them, and re-layouts  1.57 us

profile of v5, /device:TPU:1, one launch (start us, length us, event | category | flops | bytes accessed | tf_op | source)
XLA Modules:
  0.0 39.6 jit_solution(4881023038421517440)
XLA Ops:
  0.0 38.0 %signals.1 = f32[32,4,256]{2,1,0:T(4,128)} custom-call(bf16[64,8,128]{2,1,0:T(8,128)(2,1)} %sources_ref.1, s32[1,64]{1,0:T(1,128)} %bitcast.13, s32[1,64]{1,0:T(1,128)} %bitcast.14, s32[1,64]{1,0:T(1,128)} %bitcast.15, s32[1024,128]{1,0:T(8,128)} %bitcast.11, f32[1024,128]{1,0:T(8,128)} %bitcast.12, bf16[65536,128]{1,0:T(8,128)(2,1)} %bitcast.10), custom_call_target="tpu_custom_call" | custom-call | tf_op jit(solution)/shard_map/signals/pallas_call | solution.py:471
  38.0 1.6 %copy.10 = f32[32,4,256]{2,1,0:T(4,128)} copy(f32[32,4,256]{2,1,0:T(4,128)} %signals.1) | data formatting | bytes 262144

commit v6 on v5

--- a/solution.py
+++ b/solution.py
@@ -16,6 +16,7 @@
 CHUNK = 128
 SLOTS = 4
 UNROLL = 64
+CUTS = 2
 MESH = pl.DeviceIdType.MESH
 
 
@@ -44,7 +45,7 @@
     flips = (g + 1 - 2 * bit0, g + 2 - 4 * bit1)
     corner = lax.rem(g, 4)
     rows = row_sums.shape[0] // 8
-    wide = columns * share
+    wide = columns * share // CUTS
     tall = depth * wide
     half = NBIN // 2
 
@@ -76,18 +77,6 @@
     def greet(to_g, to_q):
         pl.semaphore_signal(barrier, inc=1, device_id=(to_g, to_q), device_id_type=MESH)
 
-    def others(body):
-        def one(i, c):
-            to_z, to_q = i // columns, lax.rem(i, columns)
-
-            @pl.when(jnp.logical_or(to_z != z, to_q != q))
-            def _():
-                body(i, to_z, to_q)
-
-            return c
-
-        lax.fori_loop(0, depth * columns, one, 0)
-
     def ring(body):
         def one(i, c):
             body(lax.rem(g + i, shards))
@@ -191,17 +180,6 @@
             device_id=(g, from_q),
             device_id_type=MESH,
         )
-
-    pl.semaphore_wait(barrier, shards - 1 + depth * (columns - 1))
-    turn_round = jnp.where(z * 2 < depth, shards - 1, 1)
-
-    def far_first(i, c):
-        post(lax.rem(g + i * turn_round, shards)).start()
-        return c
-
-    lax.fori_loop(1, shards, far_first, 0)
-    got_in[q, g] = posted[g]
-    beside(lambda to_q: hand(g, to_q).start())
 
     height = per * tiles_wide * group
     row = lax.broadcasted_iota(jnp.int32, (height, 256), 0)
@@ -247,6 +225,17 @@
                     o, :, t * LANES : (t + 1) * LANES
                 ].T
         return carry
+
+    pl.semaphore_wait(barrier, shards - 1 + depth * (columns - 1))
+    turn_round = jnp.where(z * 2 < depth, shards - 1, 1)
+
+    def far_first(i, c):
+        post(lax.rem(g + i * turn_round, shards)).start()
+        return c
+
+    lax.fori_loop(1, shards, far_first, 0)
+    got_in[q, g] = posted[g]
+    beside(lambda to_q: hand(g, to_q).start())
 
     lax.fori_loop(0, steps, turn, 0)
     for table in tables:
@@ -307,74 +296,110 @@
 
         lax.fori_loop(low, high, pair, 0, unroll=UNROLL)
 
-    def multiply(j, c0, c1):
+    def multiply(j, u, c0, c1):
         lhs = jnp.concatenate(
             [
-                gains[j, pl.ds(pl.multiple_of((k * 4 + c1 * 2 + c0) * wide, 8), wide), :]
+                gains[j, pl.ds(pl.multiple_of((k * 4 + c1 * 2 + c0) * wide * CUTS + u * wide, 8), wide), :]
                 for k in range(depth)
             ],
             axis=0,
         )
         return jnp.dot(lhs, arrived[...], preferred_element_type=jnp.float32)
 
-    def stage_one(j, h, part):
-        return pltpu.make_async_remote_copy(
-            src_ref=first_out.at[j, h, part],
-            dst_ref=first_in.at[j, h, part],
-            send_sem=one_send.at[j, h, part],
-            recv_sem=one_recv.at[j, h, part],
+    def stage_one(j, u, h, part):
+        return pltpu.make_async_remote_copy(
+            src_ref=first_out.at[j, u, h, part],
+            dst_ref=first_in.at[j, u, h, part],
+            send_sem=one_send.at[j, u, h, part],
+            recv_sem=one_recv.at[j, u, h, part],
             device_id=(flips[h], q),
             device_id_type=MESH,
         )
 
-    def stage_two(j, h):
-        return pltpu.make_async_remote_copy(
-            src_ref=second_out.at[j, h],
-            dst_ref=second_in.at[j, h],
-            send_sem=two_send.at[j, h],
-            recv_sem=two_recv.at[j, h],
+    def stage_two(j, u, h):
+        return pltpu.make_async_remote_copy(
+            src_ref=second_out.at[j, u, h],
+            dst_ref=second_in.at[j, u, h],
+            send_sem=two_send.at[j, u, h],
+            recv_sem=two_recv.at[j, u, h],
             device_id=(flips[1 - h], q),
             device_id_type=MESH,
         )
 
-    def stage_three(j, i, to_z, to_q):
-        return pltpu.make_async_remote_copy(
-            src_ref=third_out.at[j, i],
-            dst_ref=third_in.at[j, z * columns + q],
-            send_sem=three_send.at[j, i],
-            recv_sem=three_recv.at[j, z * columns + q],
+    def stage_three(j, to_z, to_q):
+        return pltpu.make_async_remote_copy(
+            src_ref=third_out.at[j, to_z, to_q],
+            dst_ref=third_in.at[j, z, q],
+            send_sem=three_send.at[j, to_z, to_q],
+            recv_sem=three_recv.at[j, z, q],
             device_id=(to_z * 4 + corner, to_q),
             device_id_type=MESH,
         )
 
-    def arrival(j, i):
-        return pltpu.make_async_remote_copy(
-            src_ref=third_out.at[j, i],
-            dst_ref=third_in.at[j, i],
-            send_sem=three_send.at[j, i],
-            recv_sem=three_recv.at[j, i],
-            device_id=((i // columns) * 4 + corner, lax.rem(i, columns)),
-            device_id_type=MESH,
-        )
+    def arrival(j, from_z, from_q):
+        return pltpu.make_async_remote_copy(
+            src_ref=third_out.at[j, from_z, from_q],
+            dst_ref=third_in.at[j, from_z, from_q],
+            send_sem=three_send.at[j, from_z, from_q],
+            recv_sem=three_recv.at[j, from_z, from_q],
+            device_id=(from_z * 4 + corner, from_q),
+            device_id_type=MESH,
+        )
+
+    def others(body, low, high):
+        count = high - low
+
+        def one(n, c):
+            to_z = lax.rem(z + jnp.where(z * 2 < depth, 2 * depth - 1 - n // count, 1 + n // count), depth)
+            to_q = low + lax.rem(n, count)
+
+            @pl.when(jnp.logical_or(to_z != z, to_q != q))
+            def _():
+                body(to_z, to_q)
+
+            return c
+
+        lax.fori_loop(0, depth * count, one, 0)
 
     sides = (slice(0, half), slice(half, NBIN))
-
-    def products(j):
-        got = multiply(j, 1 - bit0, 1 - bit1)
+    span = columns // CUTS
+
+    def products(j, u):
+        got = multiply(j, u, 1 - bit0, 1 - bit1)
         for h in range(2):
-            first_out[j, h, 0] = bf16(got[:, sides[h]])
-            stage_one(j, h, 0).start()
-        got = multiply(j, 1 - bit0, bit1)
-        first_out[j, 0, 1] = bf16(got[:, sides[0]])
-        stage_one(j, 0, 1).start()
-        kept[j, 1] = got[:, sides[1]]
-        got = multiply(j, bit0, 1 - bit1)
-        first_out[j, 1, 1] = bf16(got[:, sides[1]])
-        stage_one(j, 1, 1).start()
-        kept[j, 0] = got[:, sides[0]]
-        got = multiply(j, bit0, bit1)
+            first_out[j, u, h, 0] = bf16(got[:, sides[h]])
+            stage_one(j, u, h, 0).start()
+        got = multiply(j, u, 1 - bit0, bit1)
+        first_out[j, u, 0, 1] = bf16(got[:, sides[0]])
+        stage_one(j, u, 0, 1).start()
+        kept[j, u, 1] = got[:, sides[1]]
+        got = multiply(j, u, bit0, 1 - bit1)
+        first_out[j, u, 1, 1] = bf16(got[:, sides[1]])
+        stage_one(j, u, 1, 1).start()
+        kept[j, u, 0] = got[:, sides[0]]
+        got = multiply(j, u, bit0, bit1)
         for h in range(2):
-            last[j, h] = got[:, sides[h]]
+            last[j, u, h] = got[:, sides[h]]
+
+    def second(j, u):
+        for h in range(2):
+            stage_one(j, u, h, 0).wait_recv()
+            second_out[j, u, h] = bf16(kept[j, u, h] + first_in[j, u, h, 0].astype(jnp.float32))
+            stage_two(j, u, h).start()
+
+    def third(j, u):
+        for h in range(2):
+            stage_one(j, u, h, 1).wait_recv()
+            stage_two(j, u, h).wait_recv()
+            total = (
+                last[j, u, h]
+                + first_in[j, u, h, 1].astype(jnp.float32)
+                + second_in[j, u, h].astype(jnp.float32)
+            )
+            third_out[j, :, u * span : (u + 1) * span, :, sides[h]] = bf16(total).reshape(
+                depth, span, share, half
+            )
+        others(lambda to_z, to_q: stage_three(j, to_z, to_q).start(), u * span, (u + 1) * span)
 
     def relay(from_g):
         posted_by(from_g).wait_recv()
@@ -401,51 +426,40 @@
     )
     for k in range(terms):
         row_sums[pl.ds(k, rows, stride=terms), :] = summed[:, k * panels : (k + 1) * panels]
-    def second(j):
-        for h in range(2):
-            stage_one(j, h, 0).wait_recv()
-            second_out[j, h] = bf16(kept[j, h] + first_in[j, h, 0].astype(jnp.float32))
-            stage_two(j, h).start()
-
-    def third(j):
-        for h in range(2):
-            stage_one(j, h, 1).wait_recv()
-            stage_two(j, h).wait_recv()
-            total = (
-                last[j, h]
-                + first_in[j, h, 1].astype(jnp.float32)
-                + second_in[j, h].astype(jnp.float32)
-            )
-            third_out[j, :, :, sides[h]] = bf16(total).reshape(depth * columns, share, half)
-        others(lambda i, to_z, to_q: stage_three(j, i, to_z, to_q).start())
-        third_in[j, z * columns + q] = third_out[j, z * columns + q]
-
     pairs = rows // 2
     for j in range(per):
         if j == 0:
             scatter(j, 0, pairs)
         else:
             scatter(j, 0, pairs // 2)
-            second(j - 1)
+            second(j - 1, 0)
             scatter(j, pairs // 2, pairs)
-        products(j)
-        if j > 0:
-            third(j - 1)
-    second(per - 1)
-    third(per - 1)
+            for u in range(1, CUTS):
+                second(j - 1, u)
+        for u in range(CUTS):
+            products(j, u)
+            if j > 0:
+                third(j - 1, u)
+    for u in range(CUTS):
+        second(per - 1, u)
+    for u in range(CUTS):
+        third(per - 1, u)
     for j in range(per):
-        others(lambda i, to_z, to_q: arrival(j, i).wait_recv())
+        third_in[j, z, q] = third_out[j, z, q]
+    for j in range(per):
+        others(lambda from_z, from_q: arrival(j, from_z, from_q).wait_recv(), 0, columns)
         for c in range(columns):
-            total = third_in[j, c].astype(jnp.float32)
+            total = third_in[j, 0, c].astype(jnp.float32)
             for k in range(1, depth):
-                total = total + third_in[j, k * columns + c].astype(jnp.float32)
+                total = total + third_in[j, k, c].astype(jnp.float32)
             out_ref[:, c * per + j, :] = total
     for j in range(per):
-        for h in range(2):
-            for part in range(2):
-                stage_one(j, h, part).wait_send()
-            stage_two(j, h).wait_send()
-        others(lambda i, to_z, to_q: stage_three(j, i, to_z, to_q).wait_send())
+        for u in range(CUTS):
+            for h in range(2):
+                for part in range(2):
+                    stage_one(j, u, h, part).wait_send()
+                stage_two(j, u, h).wait_send()
+        others(lambda to_z, to_q: stage_three(j, to_z, to_q).wait_send(), 0, columns)
     ring(lambda to_g: post(to_g).wait_send())
     beside(lambda to_q: every(lambda from_g: hand(from_g, to_q).wait_send()))
 
@@ -458,8 +472,8 @@
     observers = gain_table.shape[3]
     per = blocks // columns
     share = observers // (shards * columns)
-    peers = shards // 4 * columns
-    tall = peers * share
+    depth = shards // 4
+    tall = depth * columns * share // CUTS
     half = NBIN // 2
     tiles_wide = observers // LANES
     wide = terms * panels + LANES
@@ -484,26 +498,26 @@
             pltpu.VMEM((rows * blocks, LANES), jnp.int32),
             pltpu.VMEM((rows * blocks, LANES), jnp.float32),
             pltpu.VMEM((rows * terms, NBIN), jnp.bfloat16),
-            pltpu.VMEM((per, 2, 2, tall, half), jnp.bfloat16),
-            pltpu.VMEM((per, 2, 2, tall, half), jnp.bfloat16),
-            pltpu.VMEM((per, 2, tall, half), jnp.float32),
-            pltpu.VMEM((per, 2, tall, half), jnp.float32),
-            pltpu.VMEM((per, 2, tall, half), jnp.bfloat16),
-            pltpu.VMEM((per, 2, tall, half), jnp.bfloat16),
-            pltpu.VMEM((per, peers, share, NBIN), jnp.bfloat16),
-            pltpu.VMEM((per, peers, share, NBIN), jnp.bfloat16),
+            pltpu.VMEM((per, CUTS, 2, 2, tall, half), jnp.bfloat16),
+            pltpu.VMEM((per, CUTS, 2, 2, tall, half), jnp.bfloat16),
+            pltpu.VMEM((per, CUTS, 2, tall, half), jnp.float32),
+            pltpu.VMEM((per, CUTS, 2, tall, half), jnp.float32),
+            pltpu.VMEM((per, CUTS, 2, tall, half), jnp.bfloat16),
+            pltpu.VMEM((per, CUTS, 2, tall, half), jnp.bfloat16),
+            pltpu.VMEM((per, depth, columns, share, NBIN), jnp.bfloat16),
+            pltpu.VMEM((per, depth, columns, share, NBIN), jnp.bfloat16),
             dma((SLOTS,)),
             dma((2,)),
             dma((shards,)),
             dma((shards,)),
             dma((columns, shards)),
             dma((columns, shards)),
-            dma((per, 2, 2)),
-            dma((per, 2, 2)),
-            dma((per, 2)),
-            dma((per, 2)),
-            dma((per, peers)),
-            dma((per, peers)),
+            dma((per, CUTS, 2, 2)),
+            dma((per, CUTS, 2, 2)),
+            dma((per, CUTS, 2)),
+            dma((per, CUTS, 2)),
+            dma((per, depth, columns)),
+            dma((per, depth, columns)),
         ],
         compiler_params=pltpu.CompilerParams(collective_id=0, has_side_effects=True),
         name="signals",

time: 39.8 us -> 39.4 us (0.990)
  no operation moved by 1% of the time
where the time goes in v6:
time: 39.4 us; the launch traced here: 39.3 us
  Pallas kernels  37.7 us (96%)
  local copies, waits for them, and re-layouts  1.57 us (4%)
    pallas_call x1, Pallas kernels, on_device(): pl.pallas_call(functools.partial(signals_kernel, per, share, cap), out_sh...  37.7 us
    unnamed x1, local copies, waits for them, and re-layouts  1.57 us

profile of v6, /device:TPU:1, one launch (start us, length us, event | category | flops | bytes accessed | tf_op | source)
XLA Modules:
  0.0 39.3 jit_solution(18154399222681528755)
XLA Ops:
  0.0 37.7 %signals.1 = f32[32,4,256]{2,1,0:T(4,128)} custom-call(bf16[64,8,128]{2,1,0:T(8,128)(2,1)} %sources_ref.1, s32[1,64]{1,0:T(1,128)} %bitcast.13, s32[1,64]{1,0:T(1,128)} %bitcast.14, s32[1,64]{1,0:T(1,128)} %bitcast.15, s32[1024,128]{1,0:T(8,128)} %bitcast.11, f32[1024,128]{1,0:T(8,128)} %bitcast.12, bf16[65536,128]{1,0:T(8,128)(2,1)} %bitcast.10), custom_call_target="tpu_custom_call" | custom-call | tf_op jit(solution)/shard_map/signals/pallas_call | solution.py:485
  37.7 1.6 %copy.10 = f32[32,4,256]{2,1,0:T(4,128)} copy(f32[32,4,256]{2,1,0:T(4,128)} %signals.1) | data formatting | bytes 262144

commit v7 on v6

--- a/solution.py
+++ b/solution.py
@@ -13,7 +13,7 @@
 LO_BITS = LO.bit_length() - 1
 HI = NBIN // LO
 WIDE = LO + 16
-CHUNK = 128
+CHUNK = 256
 SLOTS = 4
 UNROLL = 64
 CUTS = 2

time: 39.4 us -> 39.4 us (level)
  no operation moved by 1% of the time
where the time goes in v7:
time: 39.4 us; the launch traced here: 39.3 us
  Pallas kernels  37.7 us (96%)
  local copies, waits for them, and re-layouts  1.57 us (4%)
    pallas_call x1, Pallas kernels, on_device(): pl.pallas_call(functools.partial(signals_kernel, per, share, cap), out_sh...  37.7 us
    unnamed x1, local copies, waits for them, and re-layouts  1.57 us

profile of v7, /device:TPU:1, one launch (start us, length us, event | category | flops | bytes accessed | tf_op | source)
XLA Modules:
  0.0 39.3 jit_solution(75624266445376733)
XLA Ops:
  0.0 37.7 %signals.1 = f32[32,4,256]{2,1,0:T(4,128)} custom-call(bf16[64,8,128]{2,1,0:T(8,128)(2,1)} %sources_ref.1, s32[1,64]{1,0:T(1,128)} %bitcast.13, s32[1,64]{1,0:T(1,128)} %bitcast.14, s32[1,64]{1,0:T(1,128)} %bitcast.15, s32[1024,128]{1,0:T(8,128)} %bitcast.11, f32[1024,128]{1,0:T(8,128)} %bitcast.12, bf16[65536,128]{1,0:T(8,128)(2,1)} %bitcast.10), custom_call_target="tpu_custom_call" | custom-call | tf_op jit(solution)/shard_map/signals/pallas_call | solution.py:485
  37.7 1.6 %copy.10 = f32[32,4,256]{2,1,0:T(4,128)} copy(f32[32,4,256]{2,1,0:T(4,128)} %signals.1) | data formatting | bytes 262144
